TPU v7x, 32 devices: a whole 2x2x4 slice. The times are simulated.
32 devices in a mesh: data: 32 (over z, y, x, core).
Axes of the slice: x: 2, y: 2, z: 4, core: 2. Of those that a mesh axis runs over, the one named last changes fastest.
Arguments:
- tokens: bfloat16 [32768, 1280], P('data')
- targets: bfloat16 [32768, 1280], P('data')
- w_in: bfloat16 [2, 1280, 5120], replicated
- w_out: bfloat16 [2, 5120, 1280], replicated
Outputs:
- output 1: float32 [2, 1280, 5120], P(None, 'data')
- output 2: float32 [2, 5120, 1280], P(None, 'data')
All inputs are finite; a program needn't handle non-finite values.
Results may differ from a plain program's by a relative error of at most 0.00409974.
Values are sent between devices in bfloat16 or wider.
A program may use at most 1 GiB of HBM per device.

v0:
```python
import jax
import jax.numpy as jnp
from jax import lax
from jax.experimental import pallas as pl
from jax.experimental.pallas import tpu as pltpu
from jax.sharding import PartitionSpec as P


CORE, X, Y, ZL, ZH = 1, 2, 4, 8, 16
F32, BF16 = jnp.float32, jnp.bfloat16


def gelu_act(pre_f32):
    return jax.nn.gelu(pre_f32, approximate=True)


def dot(a, b, dims):
    return lax.dot_general(a, b, (dims, ((), ())), preferred_element_type=F32)


NN, NT, TN = ((1,), (0,)), ((1,), (1,)), ((0,), (0,))
ANY = pl.BlockSpec(memory_space=pl.ANY)
WHOLE = pl.BlockSpec(memory_space=pltpu.VMEM)


def grad_pre_of(pre, grad_act):
    _, pullback = jax.vjp(gelu_act, pre.astype(F32))
    return pullback(grad_act.astype(F32))[0].astype(BF16)


def start_rows(refs, buf, sems, piece):
    k = 0
    for ref in refs:
        for r in range(0, ref.shape[0], piece):
            pltpu.make_async_copy(ref.at[pl.ds(r, piece)], buf.at[pl.ds(k * piece, piece)], sems.at[k]).start()
            k += 1


def wait_rows(buf, sems, piece, tile, i):
    for j in range(tile // piece):
        k = i * (tile // piece) + j
        view = buf.at[pl.ds(k * piece, piece)]
        pltpu.make_async_copy(view, view, sems.at[k]).wait()


def call(kernel, operands, in_specs, out_shape, out_specs, scratch, flops):
    nbytes = sum(o.size * o.dtype.itemsize for o in operands)
    return pl.pallas_call(
        kernel, out_shape=out_shape, in_specs=in_specs, out_specs=out_specs, scratch_shapes=scratch,
        compiler_params=pltpu.CompilerParams(vmem_limit_bytes=62 * 1024 * 1024),
        cost_estimate=pl.CostEstimate(flops=flops, bytes_accessed=nbytes, transcendentals=0),
    )(*operands)


def sizes_of(blocks):
    piece = min(b.shape[0] for b in blocks)
    total = sum(b.shape[0] for b in blocks)
    return piece, total, blocks[0].shape[1]


def share_forward(blocks, w):
    piece, total, d = sizes_of(blocks)
    cols = w.shape[1]
    nb, steps = len(blocks), total // piece

    def kernel(*refs):
        h_refs, (w_ref, pre_ref, act_ref, h_buf, pre_buf, act_buf, sems, out_sems) = refs[:nb], refs[nb:]
        start_rows(h_refs, h_buf, sems, piece)

        def outs(i, slot):
            rows = pl.ds(i * piece, piece)
            return (pltpu.make_async_copy(pre_buf.at[slot], pre_ref.at[rows], out_sems.at[slot, 0]),
                    pltpu.make_async_copy(act_buf.at[slot], act_ref.at[rows], out_sems.at[slot, 1]))

        def step(i, _):
            slot = i % 2
            wait_rows(h_buf, sems, piece, piece, i)

            @pl.when(i >= 2)
            def _():
                for c in outs(i - 2, slot):
                    c.wait()

            pre = dot(h_buf[pl.ds(i * piece, piece), :], w_ref[...], NN).astype(BF16)
            pre_buf[slot] = pre
            act_buf[slot] = gelu_act(pre.astype(F32)).astype(BF16)
            for c in outs(i, slot):
                c.start()
            return 0

        lax.fori_loop(0, steps, step, 0)
        for i in range(max(steps - 2, 0), steps):
            for c in outs(i, i % 2):
                c.wait()

    shape = jax.ShapeDtypeStruct((total, cols), BF16)
    return call(kernel, [*blocks, w], [ANY] * nb + [WHOLE], [shape, shape], [ANY, ANY],
                [pltpu.VMEM((total, d), BF16), pltpu.VMEM((2, piece, cols), BF16), pltpu.VMEM((2, piece, cols), BF16),
                 pltpu.SemaphoreType.DMA((steps,)), pltpu.SemaphoreType.DMA((2, 2))], 2 * total * d * cols)


def share_out(act, blocks):
    piece, total, d = sizes_of(blocks)
    cols = act.shape[1]
    nb, tile = len(blocks), 2 * piece

    def kernel(*refs):
        act_ref, g_refs, (out_ref, act_buf, g_buf, act_sems, sems) = refs[0], refs[1:1 + nb], refs[1 + nb:]
        start_rows([act_ref], act_buf, act_sems, piece)
        start_rows(g_refs, g_buf, sems, piece)
        chunk = cols // 5 if cols % 640 == 0 else cols

        def step(i, _):
            wait_rows(act_buf, act_sems, piece, tile, i)
            wait_rows(g_buf, sems, piece, tile, i)
            rows = pl.ds(i * tile, tile)

            def part(c, _):
                at = pl.ds(pl.multiple_of(c * chunk, chunk), chunk)
                val = dot(act_buf[rows, at], g_buf[rows, :], TN)

                @pl.when(i == 0)
                def _():
                    out_ref[at, :] = val

                @pl.when(i > 0)
                def _():
                    out_ref[at, :] += val

                return 0

            lax.fori_loop(0, cols // chunk, part, 0)
            return 0

        lax.fori_loop(0, total // tile, step, 0)

    return call(kernel, [act, *blocks], [ANY] * (nb + 1), jax.ShapeDtypeStruct((cols, d), F32), WHOLE,
                [pltpu.VMEM((total, cols), BF16), pltpu.VMEM((total, d), BF16),
                 pltpu.SemaphoreType.DMA((total // piece,)), pltpu.SemaphoreType.DMA((total // piece,))],
                2 * total * d * cols)


def share_in(hs, gs, pre, w):
    piece, total, d = sizes_of(hs)
    cols = w.shape[0]
    nb, tile = len(hs), 2 * piece
    steps = total // tile

    def kernel(*refs):
        h_refs, g_refs = refs[:nb], refs[nb:2 * nb]
        pre_ref, w_ref, out_ref, h_buf, g_buf, pre_buf, v_buf, h_sems, g_sems, pre_sems = refs[2 * nb:]
        start_rows(g_refs, g_buf, g_sems, piece)
        start_rows(h_refs, h_buf, h_sems, piece)

        def fetch(i, slot):
            return pltpu.make_async_copy(pre_ref.at[pl.ds(i * tile, tile)], pre_buf.at[slot], pre_sems.at[slot])

        fetch(0, 0).start()
        chunk = d // 5 if d % 640 == 0 else d

        def step(i, _):
            slot = i % 2
            wait_rows(g_buf, g_sems, piece, tile, i)
            wait_rows(h_buf, h_sems, piece, tile, i)
            fetch(i, slot).wait()

            @pl.when(i + 1 < steps)
            def _():
                fetch(i + 1, 1 - slot).start()

            def head(j, _):
                sub = pl.ds(j * piece, piece)
                e = dot(g_buf[pl.ds(i * tile + j * piece, piece), :], w_ref[...], NT).astype(BF16)
                v_buf[sub, :] = grad_pre_of(pre_buf[slot, sub, :], e)
                return 0

            lax.fori_loop(0, 2, head, 0)
            rows = pl.ds(i * tile, tile)

            def part(c, _):
                at = pl.ds(pl.multiple_of(c * chunk, chunk), chunk)
                val = dot(h_buf[rows, at], v_buf[...], TN)

                @pl.when(i == 0)
                def _():
                    out_ref[at, :] = val

                @pl.when(i > 0)
                def _():
                    out_ref[at, :] += val

                return 0

            lax.fori_loop(0, d // chunk, part, 0)
            return 0

        lax.fori_loop(0, steps, step, 0)

    n_sem = total // piece
    return call(kernel, [*hs, *gs, pre, w], [ANY] * (2 * nb + 1) + [WHOLE], jax.ShapeDtypeStruct((d, cols), F32), WHOLE,
                [pltpu.VMEM((total, d), BF16), pltpu.VMEM((total, d), BF16), pltpu.VMEM((2, tile, cols), BF16),
                 pltpu.VMEM((tile, cols), BF16), pltpu.SemaphoreType.DMA((n_sem,)), pltpu.SemaphoreType.DMA((n_sem,)),
                 pltpu.SemaphoreType.DMA((2,))], 4 * total * d * cols)


def solution(mesh):
    n = mesh.shape["data"]

    def permute(v, pairs):
        return lax.ppermute(v, "data", pairs)

    def swap(v, bit):
        return permute(v, [(i, i ^ bit) for i in range(n)])

    def local_grads(tokens, targets, w_in, w_out):
        rows, d = tokens.shape
        ff = w_in.shape[2]
        dr, fr = d // n, ff // n
        scale = (rows * n) ** -0.5
        idx = lax.axis_index("data")

        def bit(b):
            return (idx // b) % 2

        z = idx // 8

        def plane_gather(v):
            vx, vy = swap(v, X), swap(v, Y)
            half = rows // 2
            lo = swap(vx[:half], Y)
            hi = swap(vy[half:], X)
            mine = [v, vx, vy, lo, hi]
            return mine + [swap(m, CORE) for m in mine]

        def pair_gather(v):
            mine = [v, swap(v, ZL)]
            return mine + [swap(m, CORE) for m in mine]

        def halve(arr, axis, b):
            keep = lax.dynamic_index_in_dim(arr, bit(b), axis, keepdims=False)
            send = lax.dynamic_index_in_dim(arr, 1 - bit(b), axis, keepdims=False)
            return keep + swap(send, b)

        def line_reduce(arr):
            right = [[(i, i + 8) for i in range(n) if i // 8 <= min(s, 2)] for s in range(3)]
            left = [[(i, i - 8) for i in range(n) if 3 - i // 8 <= min(s, 2)] for s in range(3)]
            recv_r = recv_l = None
            for s in range(3):
                send_r = lax.dynamic_index_in_dim(arr, jnp.clip(3 - s + z, 0, 3), 0, keepdims=False)
                send_l = lax.dynamic_index_in_dim(arr, jnp.clip(s + z - 3, 0, 3), 0, keepdims=False)
                if s:
                    send_r, send_l = send_r + recv_r, send_l + recv_l
                recv_r = permute(send_r, right[s])
                recv_l = permute(send_l, left[s])
            own = lax.dynamic_index_in_dim(arr, z, 0, keepdims=False)
            return own + recv_r + recv_l

        def spread(arr, axis, b):
            keep = lax.dynamic_index_in_dim(arr, bit(b), axis, keepdims=False)
            send = lax.dynamic_index_in_dim(arr, 1 - bit(b), axis, keepdims=False)
            recv = swap(send, b)
            first = jnp.where(bit(b) == 0, keep, recv)
            second = jnp.where(bit(b) == 0, recv, keep)
            return jnp.stack([first, second], axis=axis)

        def share_of(w, layer, axis, owners):
            start = lambda o: (layer, o * fr, 0) if axis == 0 else (layer, 0, o * fr)
            size = (1, fr, d) if axis == 0 else (1, d, fr)
            return jnp.concatenate([lax.dynamic_slice(w, start(o), size)[0] for o in owners], axis=axis)

        owners1 = [(zh * 16 + y * 4 + x * 2) + bit(ZL) * 8 + bit(CORE)
                   for zh in range(2) for y in range(2) for x in range(2)]
        owners0 = [zz * 8 + idx % 8 for zz in range(4)]

        h0s = plane_gather(tokens)
        pre0 = dot(tokens, w_in[0], NN).astype(BF16)
        act0 = gelu_act(pre0.astype(F32)).astype(BF16)
        h1 = (tokens.astype(F32) + dot(act0, w_out[0], NN)).astype(BF16)
        h1s = pair_gather(h1)
        pre1 = dot(h1, w_in[1], NN).astype(BF16)
        act1 = gelu_act(pre1.astype(F32)).astype(BF16)
        h2 = (h1.astype(F32) + dot(act1, w_out[1], NN)).astype(BF16)
        g1 = ((h2.astype(F32) - targets.astype(F32)) * scale).astype(BF16)
        g1s = pair_gather(g1)
        grad_act1 = dot(g1, w_out[1], NT).astype(BF16)
        grad_pre1 = grad_pre_of(pre1, grad_act1)
        g0 = (g1.astype(F32) + dot(grad_pre1, w_in[1], NT)).astype(BF16)
        g0s = plane_gather(g0)

        w_in1, w_in0 = share_of(w_in, 1, 1, owners1), share_of(w_in, 0, 1, owners0)
        w_out1, w_out0 = share_of(w_out, 1, 0, owners1), share_of(w_out, 0, 0, owners0)
        pre1s, act1s = share_forward(h1s, w_in1)
        pre0s, act0s = share_forward(h0s, w_in0)
        out1 = share_out(act1s, g1s)
        in1 = share_in(h1s, g1s, pre1s, w_out1)
        in0 = share_in(h0s, g0s, pre0s, w_out0)
        out0 = share_out(act0s, g0s)

        out1 = out1.reshape(2, 2, 2, fr, d)
        out1 = halve(out1, 2, X)
        out1 = halve(out1, 1, Y)
        out1 = halve(out1, 0, ZH)
        in1 = in1.reshape(2, 2, 2, 2, 2, dr, 8 * fr)
        in1 = halve(in1, 2, Y)
        in1 = halve(in1, 2, X)
        in1 = halve(in1, 0, ZH)
        in1 = spread(spread(in1, 0, ZL), 1, CORE)
        in1 = in1.reshape(2, 2, dr, 2, 2, 2, fr)
        in1 = in1.transpose(2, 3, 0, 4, 5, 1, 6).reshape(dr, ff)

        out0 = line_reduce(out0.reshape(4, fr, d))
        in0 = line_reduce(in0.reshape(4, 8 * dr, 4 * fr))
        in0 = in0.reshape(2, 2, 2, dr, 4 * fr)
        in0 = spread(spread(spread(in0, 0, Y), 1, X), 2, CORE)
        in0 = in0.reshape(8, dr, 4, fr).transpose(1, 2, 0, 3).reshape(dr, ff)
        return jnp.stack([in0, in1]), jnp.stack([out0, out1])

    tok_spec = P("data", None)
    grad_spec = P(None, "data", None)
    return jax.shard_map(local_grads, mesh=mesh, in_specs=(tok_spec, tok_spec, P(), P()), out_specs=(grad_spec, grad_spec), check_vma=False)
```

profile of v0, /device:TPU:14, one launch (start us, length us, event | category | flops | bytes accessed | tf_op | source)
XLA Modules:
  0.0 757.4 jit_solution(15564879669583363656)
XLA Ops:
  1.7 20.1 %fusion.141 = bf16[1024,5120]{1,0:T(8,128)(2,1)S(1)} fusion(bf16[1024,1280]{1,0:T(8,128)(2,1)} %refs_0_.3, bf16[2,1280,5120]{2,1,0:T(8,128)(2,1)} %param.6), kind=kOutput, calls=%fused_computation.20.clone.clone.clone.clone.2 | convolution fusion | flops 13479444480 | bytes 26214400 | tf_op jit(solution)/shard_map/dot_general | solution.py:18
  21.8 17.1 %add_convert_fusion.2.refs_0_ = bf16[1024,1280]{1,0:T(8,128)(2,1)} fusion(bf16[1024,1280]{1,0:T(8,128)(2,1)} %refs_0_.3, bf16[2,5120,1280]{2,1,0:T(8,128)(2,1)} %param.7, bf16[1024,5120]{1,0:T(8,128)(2,1)S(1)} %fusion.141), kind=kOutput, calls=%fused_computation.56 | convolution fusion | flops 13425704960 | bytes 28835840 | tf_op jit(solution)/shard_map/dot_general | solution.py:18
  39.0 19.9 %fusion.49 = bf16[1024,5120]{1,0:T(8,128)(2,1)} fusion(bf16[1024,1280]{1,0:T(8,128)(2,1)} %add_convert_fusion.2.refs_0_, bf16[2,1280,5120]{2,1,0:T(8,128)(2,1)} %param.6), kind=kOutput, calls=%fused_computation.52 | convolution fusion | flops 13427015680 | bytes 26214400 | tf_op jit(solution)/shard_map/dot_general | solution.py:18
  58.9 26.7 %multiply_convert_fusion.refs_4_.refs_1_ = bf16[1024,1280]{1,0:T(8,128)(2,1)} fusion(bf16[1024,1280]{1,0:T(8,128)(2,1)S(1)} %copy-done.4, bf16[2,5120,1280]{2,1,0:T(8,128)(2,1)} %param.7, bf16[1024,5120]{1,0:T(8,128)(2,1)} %fusion.49, bf16[1024,1280]{1,0:T(8,128)(2,1)} %add_convert_fusion.2.refs_0_), kind=kOutput, calls=%fused_computation.54 | convolution fusion | flops 13484687360 | bytes 31457280 | tf_op jit(solution)/shard_map/dot_general | solution.py:18
  85.6 1.9 collective-permute-start.30
  87.5 29.5 %fusion.137 = bf16[1024,5120]{1,0:T(8,128)(2,1)} fusion(bf16[1024,5120]{1,0:T(8,128)(2,1)} %fusion.49, bf16[1024,1280]{1,0:T(8,128)(2,1)} %multiply_convert_fusion.refs_4_.refs_1_, bf16[2,5120,1280]{2,1,0:T(8,128)(2,1)} %param.7), kind=kOutput, calls=%fused_computation.13.clone.clone.clone.clone.2 | convolution fusion | flops 13542359040 | bytes 36700160 | tf_op jit(solution)/shard_map/dot_general | solution.py:18
  117.0 21.2 %add_convert_fusion.refs_10_.refs_1_ = bf16[1024,1280]{1,0:T(8,128)(2,1)} fusion(bf16[1024,1280]{1,0:T(8,128)(2,1)S(1)} %copy-done.5, bf16[2,1280,5120]{2,1,0:T(8,128)(2,1)} %param.6, bf16[1024,5120]{1,0:T(8,128)(2,1)} %fusion.137), kind=kOutput, calls=%fused_computation.53 | convolution fusion | flops 13425704960 | bytes 28835840 | tf_op jit(solution)/shard_map/dot_general | solution.py:18
  139.8 1.6 collective-permute-start.10
  141.4 2.5 slice.34
  143.8 9.7 %collective-permute-done.30.refs_5_.refs_2_ = bf16[1024,1280]{1,0:T(8,128)(2,1)} collective-permute-done((bf16[1024,1280]{1,0:T(8,128)(2,1)}, bf16[1024,1280]{1,0:T(8,128)(2,1)}, u32[]{:S(2)}, u32[]{:S(2)}) %collective-permute-start.30) | collective-permute-done | bytes 2621472 | tf_op jit(solution)/shard_map/ppermute | solution.py:210
  155.0 42.6 %collective-permute-done.9.refs_11_.refs_2_ = bf16[1024,1280]{1,0:T(8,128)(2,1)} collective-permute-done((bf16[1024,1280]{1,0:T(8,128)(2,1)}, bf16[1024,1280]{1,0:T(8,128)(2,1)}, u32[]{:S(2)}, u32[]{:S(2)}) %collective-permute-start.9) | collective-permute-done | bytes 2621472 | tf_op jit(solution)/shard_map/ppermute | solution.py:210
  197.6 1.8 bitcast_dynamic-update-slice_fusion.7
  205.3 1.8 bitcast_dynamic-update-slice_fusion.6
  207.1 2.5 slice.37
  209.6 18.4 %collective-permute-done.2.refs_3_ = bf16[512,1280]{1,0:T(8,128)(2,1)} collective-permute-done((bf16[512,1280]{1,0:T(8,128)(2,1)}, bf16[512,1280]{1,0:T(8,128)(2,1)}, u32[]{:S(2)}, u32[]{:S(2)}) %collective-permute-start.2) | collective-permute-done | bytes 1310752 | tf_op jit(solution)/shard_map/ppermute | solution.py:210
  228.5 1.8 bitcast_dynamic-update-slice_fusion.5
  230.3 1.8 bitcast_dynamic-update-slice_fusion.4
  232.1 1.8 bitcast_dynamic-update-slice_fusion.3
  233.9 1.8 bitcast_dynamic-update-slice_fusion.2
  237.3 18.3 %collective-permute-done.11.refs_13_.refs_4_ = bf16[512,1280]{1,0:T(8,128)(2,1)} collective-permute-done((bf16[512,1280]{1,0:T(8,128)(2,1)S(1)}, bf16[512,1280]{1,0:T(8,128)(2,1)}, u32[]{:S(2)}, u32[]{:S(2)}) %collective-permute-start.11) | collective-permute-done | bytes 1310752 | tf_op jit(solution)/shard_map/ppermute | solution.py:210
  255.5 1.8 bitcast_dynamic-update-slice_fusion.1
  257.3 4.4 collective-permute-done.12.refs_14_.refs_5_
  262.3 9.9 %dynamic-slice_bitcast_fusion.21 = (bf16[1280,160]{1,0:T(8,128)(2,1)S(1)}, bf16[1280,160]{1,0:T(8,128)(2,1)S(1)}, bf16[1280,160]{1,0:T(8,128)(2,1)S(1)}, bf16[12...) fusion(bf16[2,1280,5120]{2,1,0:T(8,128)(2,1)} %param.6, ...), kind=kLoop, calls=%fused_computation.116 | loop fusion | bytes 9830448 | tf_op jit(solution)/shard_map/squeeze | solution.py:269
  272.2 2.4 pad_maximum_fusion.refs_10_
  276.4 1.8 bitcast_dynamic-update-slice_fusion.refs_9_
  278.1 7.8 %concatenate.15.refs_4_ = bf16[1280,1280]{1,0:T(8,128)(2,1)} concatenate(bf16[1280,160]{1,0:T(8,128)(2,1)} %get-tuple-element.20, bf16[1280,160]{1,0:T(8,128)(2,1)S(1)} %get-tuple-element.19, bf16[1280,160]{1,0:T(8,128)(2,1)S(1)} %get-tuple-element.18, bf16[1280,160]{1,0:T(8,128)(2,1)S(1)} %get-tuple-element.17, bf16[1280,160]{1,0:T(8,128)(2,1)S(1)} %get-tuple-element.16, ...), dimensions={1} | concatenate | bytes 6553600 | tf_op jit(solution)/shard_map/concatenate | solution.py:269
  285.9 25.9 %shard_map.59 = (bf16[8192,640]{1,0:T(8,128)(2,1)}, bf16[8192,640]{1,0:T(8,128)(2,1)}) custom-call(bf16[1024,1280]{1,0:T(8,128)(2,1)} %refs_0_.3, bf16[1024,1280]{1,0:T(8,128)(2,1)} %collective-permute-done.refs_1_, bf16[1024,1280]{1,0:T(8,128)(2,1)} %collective-permute-done.1.refs_2_, bf16[512,1280]{1,0:T(8,128)(2,1)} %collective-permute-done.2.refs_3_, ...), custom_call_target="tpu_custom_call" | custom-call | flops 13421772800 | bytes 22609920 | tf_op jit(solution)/shard_map/pallas_call | solution.py:48
  313.0 72.7 %shard_map.60 = f32[1280,640]{1,0:T(8,128)} custom-call(bf16[1024,1280]{1,0:T(8,128)(2,1)} %refs_0_.3, bf16[1024,1280]{1,0:T(8,128)(2,1)} %collective-permute-done.refs_1_, bf16[1024,1280]{1,0:T(8,128)(2,1)} %collective-permute-done.1.refs_2_, bf16[512,1280]{1,0:T(8,128)(2,1)} %collective-permute-done.2.refs_3_, ...), custom_call_target="tpu_custom_call" | custom-call | flops 26843545600 | bytes 54067200 | tf_op jit(solution)/shard_map/pallas_call | solution.py:48
  387.2 1.8 collective-permute-start.18
  389.0 28.8 %shard_map.63 = f32[640,1280]{1,0:T(8,128)} custom-call(bf16[8192,640]{1,0:T(8,128)(2,1)} %get-tuple-element.8.refs_0_, bf16[1024,1280]{1,0:T(8,128)(2,1)} %add_convert_fusion.refs_10_.refs_1_, bf16[1024,1280]{1,0:T(8,128)(2,1)} %collective-permute-done.9.refs_11_.refs_2_, bf16[1024,1280]{1,0:T(8,128)(2,1)} %collective-permute-done.10.refs_12_.refs_3_, ...), custom_call_target="tpu_custom_call" | custom-call | flops 13421772800 | bytes 31457280 | tf_op jit(solution)/shard_map/pallas_call | solution.py:48
  417.8 2.8 dynamic-slice_bitcast_fusion.6
  421.8 23.9 %shard_map.61 = (bf16[4096,1280]{1,0:T(8,128)(2,1)}, bf16[4096,1280]{1,0:T(8,128)(2,1)}) custom-call(bf16[1024,1280]{1,0:T(8,128)(2,1)} %add_convert_fusion.2.refs_0_, bf16[1024,1280]{1,0:T(8,128)(2,1)} %collective-permute-done.27.refs_1_, bf16[1024,1280]{1,0:T(8,128)(2,1)} %collective-permute-done.28.refs_2_, ...), custom_call_target="tpu_custom_call" | custom-call | flops 13421772800 | bytes 13762560 | tf_op jit(solution)/shard_map/pallas_call | solution.py:48
  445.7 55.5 %shard_map.62 = f32[1280,1280]{1,0:T(8,128)} custom-call(bf16[1024,1280]{1,0:T(8,128)(2,1)} %add_convert_fusion.2.refs_0_, bf16[1024,1280]{1,0:T(8,128)(2,1)} %collective-permute-done.27.refs_1_, bf16[1024,1280]{1,0:T(8,128)(2,1)} %collective-permute-done.28.refs_2_, bf16[1024,1280]{1,0:T(8,128)(2,1)} %collective-permute-done.29.refs_3_, ...), custom_call_target="tpu_custom_call" | custom-call | flops 26843545600 | bytes 34734080 | tf_op jit(solution)/shard_map/pallas_call | solution.py:48
  501.3 3.9 dynamic-slice_bitcast_fusion.1
  505.2 1.6 collective-permute-start.33
  509.9 2.4 bitcast_add_fusion.13
  512.3 3.8 collective-permute-start.19
  516.1 2.4 bitcast_add_fusion.7
  518.5 1.9 collective-permute-start.39
  520.5 23.5 %shard_map.64 = f32[1280,1280]{1,0:T(8,128)} custom-call(bf16[4096,1280]{1,0:T(8,128)(2,1)} %get-tuple-element.9.refs_0_, bf16[1024,1280]{1,0:T(8,128)(2,1)} %multiply_convert_fusion.refs_4_.refs_1_, bf16[1024,1280]{1,0:T(8,128)(2,1)} %collective-permute-done.30.refs_5_.refs_2_, bf16[1024,1280]{1,0:T(8,128)(2,1)} %collective-permute-done.31.refs_6_.refs_3_, ...), custom_call_target="tpu_custom_call" | custom-call | flops 13421772800 | bytes 20971520 | tf_op jit(solution)/shard_map/pallas_call | solution.py:48
  544.0 3.0 bitcast_add_fusion.14
  548.3 4.1 dynamic-slice_bitcast_fusion
  553.9 4.8 collective-permute-start.20
  558.7 1.6 bitcast_add_fusion.8
  561.6 8.7 %collective-permute-done.22 = f32[320,640]{1,0:T(8,128)} collective-permute-done((f32[320,640]{1,0:T(8,128)}, f32[320,640]{1,0:T(8,128)}, u32[]{:S(2)}, u32[]{:S(2)}) %collective-permute-start.22) | collective-permute-done | bytes 819232 | tf_op jit(solution)/shard_map/ppermute | solution.py:210
  570.3 2.2 collective-permute-start.40
  573.7 4.9 collective-permute-done.33
  578.6 6.1 collective-permute-start.23
  584.7 3.3 bitcast_add_fusion.1
  589.8 14.3 %collective-permute-done.23 = f32[320,640]{1,0:T(8,128)S(1)} collective-permute-done((f32[320,640]{1,0:T(8,128)S(1)}, f32[320,640]{1,0:T(8,128)S(1)}, u32[]{:S(2)}, u32[]{:S(2)}) %collective-permute-start.23) | collective-permute-done | bytes 819232 | tf_op jit(solution)/shard_map/ppermute | solution.py:210
  605.0 3.0 collective-permute-start.43
  608.0 6.8 collective-permute-done.24
  616.2 10.2 %collective-permute-done.44 = f32[2,2,160,1280]{3,2,1,0:T(8,128)} collective-permute-done((f32[2,2,160,1280]{3,2,1,0:T(8,128)}, f32[2,2,160,1280]{3,2,1,0:T(8,128)}, u32[]{:S(2)}, u32[]{:S(2)}) %collective-permute-start.44) | collective-permute-done | bytes 3276832 | tf_op jit(solution)/shard_map/ppermute | solution.py:210
  626.5 2.4 bitcast_add_fusion
  629.5 39.6 %collective-permute-done.25 = f32[2,2,40,640]{3,2,0,1:T(8,128)S(1)} collective-permute-done((f32[2,2,40,640]{3,2,0,1:T(8,128)S(1)}, f32[2,2,40,640]{3,2,0,1:T(8,128)S(1)}, u32[]{:S(2)}, u32[]{:S(2)}) %collective-permute-start.25) | collective-permute-done | bytes 409632 | tf_op jit(solution)/shard_map/ppermute | solution.py:210
  669.4 3.3 collective-permute-start.35
  674.6 32.0 %collective-permute-done.35 = f32[2,2,40,1280]{3,2,1,0:T(8,128)S(1)} collective-permute-done((f32[2,2,40,1280]{3,2,1,0:T(8,128)S(1)}, f32[2,2,40,1280]{3,2,1,0:T(8,128)S(1)}, u32[]{:S(2)}, u32[]{:S(2)}) %collective-permute-start.35) | collective-permute-done | bytes 819232 | tf_op jit(solution)/shard_map/ppermute | solution.py:210
  707.6 2.5 collective-permute-start.36
  713.3 2.0 reshape.29
  715.3 1.8 copy.13
  717.2 2.2 stack_reshape.6
  719.4 7.1 collective-permute-done.36
  727.8 20.1 %collective-permute-done.46 = f32[160,1280]{1,0:T(8,128)} collective-permute-done((f32[160,1280]{1,0:T(8,128)}, f32[160,1280]{1,0:T(8,128)}, u32[]{:S(2)}, u32[]{:S(2)}) %collective-permute-start.46) | collective-permute-done | bytes 819232 | tf_op jit(solution)/shard_map/ppermute | solution.py:210
  754.1 1.8 stack_reshape.7
  (119 shorter events, 46.7 us)
Async XLA Ops:
  0.6 139.2 %collective-permute-start = (bf16[1024,1280]{1,0:T(8,128)(2,1)}, bf16[1024,1280]{1,0:T(8,128)(2,1)}, u32[]{:S(2)}, u32[]{:S(2)}) collective-permute-start(bf16[1024,1280]{1,0:T(8,128)(2,1)} %refs_0_.3), channel_id=1, source_target_pairs={{0,2},{1,3},{2,0},{3,1},{4,6},{5,7},{6,4},{7,5},{8,10},{9,11},{10,... | collective-permute-start | bytes 7864328 | tf_op jit(solution)/shard_map/ppermute | solution.py:210
  1.2 153.8 %collective-permute-start.1 = (bf16[1024,1280]{1,0:T(8,128)(2,1)}, bf16[1024,1280]{1,0:T(8,128)(2,1)}, u32[]{:S(2)}, u32[]{:S(2)}) collective-permute-start(bf16[1024,1280]{1,0:T(8,128)(2,1)} %refs_0_.3), channel_id=1, source_target_pairs={{0,4},{1,5},{2,6},{3,7},{4,0},{5,1},{6,2},{7,3},{8,12},{9,13},{10,... | collective-permute-start | bytes 7864328 | tf_op jit(solution)/shard_map/ppermute | solution.py:210
  39.0 20.0 %copy-start.4 = (bf16[1024,1280]{1,0:T(8,128)(2,1)S(1)}, bf16[1024,1280]{1,0:T(8,128)(2,1)}, u32[]{:S(2)}) copy-start(bf16[1024,1280]{1,0:T(8,128)(2,1)} %param.5) | copy-start | bytes 7864324
  39.0 100.8 %collective-permute-start.27 = (bf16[1024,1280]{1,0:T(8,128)(2,1)}, bf16[1024,1280]{1,0:T(8,128)(2,1)}, u32[]{:S(2)}, u32[]{:S(2)}) collective-permute-start(bf16[1024,1280]{1,0:T(8,128)(2,1)} %add_convert_fusion.2.refs_0_), channel_id=1, source_target_pairs={{0,8},{1,9},{2,10},{3,11},{4,12},{5,13},{6,14},{7,15},{8,0},{9,1},... | collective-permute-start | bytes 7864328 | tf_op jit(solution)/shard_map/ppermute | solution.py:210
  85.6 31.4 %copy-start.5 = (bf16[1024,1280]{1,0:T(8,128)(2,1)S(1)}, bf16[1024,1280]{1,0:T(8,128)(2,1)}, u32[]{:S(2)}) copy-start(bf16[1024,1280]{1,0:T(8,128)(2,1)} %multiply_convert_fusion.refs_4_.refs_1_) | copy-start | bytes 7864324
  85.6 67.9 %collective-permute-start.30 = (bf16[1024,1280]{1,0:T(8,128)(2,1)}, bf16[1024,1280]{1,0:T(8,128)(2,1)}, u32[]{:S(2)}, u32[]{:S(2)}) collective-permute-start(bf16[1024,1280]{1,0:T(8,128)(2,1)} %multiply_convert_fusion.refs_4_.refs_1_), channel_id=1, source_target_pairs={{0,8},{1,9},{2,10},{3,11},{4,12},{5,13},{6,14},{7,15},{8,0},{9,1},... | collective-permute-start | bytes 7864328 | tf_op jit(solution)/shard_map/ppermute | solution.py:210
  138.2 59.4 %collective-permute-start.9 = (bf16[1024,1280]{1,0:T(8,128)(2,1)}, bf16[1024,1280]{1,0:T(8,128)(2,1)}, u32[]{:S(2)}, u32[]{:S(2)}) collective-permute-start(bf16[1024,1280]{1,0:T(8,128)(2,1)} %add_convert_fusion.refs_10_.refs_1_), channel_id=1, source_target_pairs={{0,2},{1,3},{2,0},{3,1},{4,6},{5,7},{6,4},{7,5},{8,10},{9,11},{10,... | collective-permute-start | bytes 7864328 | tf_op jit(solution)/shard_map/ppermute | solution.py:210
  139.8 62.5 %collective-permute-start.4 = (bf16[1024,1280]{1,0:T(8,128)(2,1)}, bf16[1024,1280]{1,0:T(8,128)(2,1)}, u32[]{:S(2)}, u32[]{:S(2)}) collective-permute-start(bf16[1024,1280]{1,0:T(8,128)(2,1)} %refs_0_.3), channel_id=1, source_target_pairs={{0,1},{1,0},{2,3},{3,2},{4,5},{5,4},{6,7},{7,6},{8,9},{9,8},{10,11... | collective-permute-start | bytes 7864328 | tf_op jit(solution)/shard_map/ppermute | solution.py:210
  139.8 64.0 %collective-permute-start.10 = (bf16[1024,1280]{1,0:T(8,128)(2,1)}, bf16[1024,1280]{1,0:T(8,128)(2,1)}, u32[]{:S(2)}, u32[]{:S(2)}) collective-permute-start(bf16[1024,1280]{1,0:T(8,128)(2,1)} %add_convert_fusion.refs_10_.refs_1_), channel_id=1, source_target_pairs={{0,4},{1,5},{2,6},{3,7},{4,0},{5,1},{6,2},{7,3},{8,12},{9,13},{10,... | collective-permute-start | bytes 7864328 | tf_op jit(solution)/shard_map/ppermute | solution.py:210
  153.5 74.5 %collective-permute-start.2 = (bf16[512,1280]{1,0:T(8,128)(2,1)}, bf16[512,1280]{1,0:T(8,128)(2,1)}, u32[]{:S(2)}, u32[]{:S(2)}) collective-permute-start(bf16[512,1280]{1,0:T(8,128)(2,1)} %slice.34), channel_id=1, source_target_pairs={{0,4},{1,5},{2,6},{3,7},{4,0},{5,1},{6,2},{7,3},{8,12},{9,13},{10,... | collective-permute-start | bytes 3932168 | tf_op jit(solution)/shard_map/ppermute | solution.py:210
  155.0 106.7 %collective-permute-start.5 = (bf16[1024,1280]{1,0:T(8,128)(2,1)}, bf16[1024,1280]{1,0:T(8,128)(2,1)}, u32[]{:S(2)}, u32[]{:S(2)}) collective-permute-start(bf16[1024,1280]{1,0:T(8,128)(2,1)} %collective-permute-done.refs_1_), channel_id=1, source_target_pairs={{0,1},{1,0},{2,3},{3,2},{4,5},{5,4},{6,7},{7,6},{8,9},{9,8},{10,11... | collective-permute-start | bytes 7864328 | tf_op jit(solution)/shard_map/ppermute | solution.py:210
  197.6 64.6 %collective-permute-start.6 = (bf16[1024,1280]{1,0:T(8,128)(2,1)}, bf16[1024,1280]{1,0:T(8,128)(2,1)}, u32[]{:S(2)}, u32[]{:S(2)}) collective-permute-start(bf16[1024,1280]{1,0:T(8,128)(2,1)} %collective-permute-done.1.refs_2_), channel_id=1, source_target_pairs={{0,1},{1,0},{2,3},{3,2},{4,5},{5,4},{6,7},{7,6},{8,9},{9,8},{10,11... | collective-permute-start | bytes 7864328 | tf_op jit(solution)/shard_map/ppermute | solution.py:210
  202.2 34.9 %collective-permute-start.3 = (bf16[512,1280]{1,0:T(8,128)(2,1)S(1)}, bf16[512,1280]{1,0:T(8,128)(2,1)}, u32[]{:S(2)}, u32[]{:S(2)}) collective-permute-start(bf16[512,1280]{1,0:T(8,128)(2,1)S(1)} %slice.35), channel_id=1, source_target_pairs={{0,2},{1,3},{2,0},{3,1},{4,6},{5,7},{6,4},{7,5},{8,10},{9,11},{10,... | collective-permute-start | bytes 3932168 | tf_op jit(solution)/shard_map/ppermute | solution.py:210
  203.8 51.7 %collective-permute-start.11 = (bf16[512,1280]{1,0:T(8,128)(2,1)S(1)}, bf16[512,1280]{1,0:T(8,128)(2,1)}, u32[]{:S(2)}, u32[]{:S(2)}) collective-permute-start(bf16[512,1280]{1,0:T(8,128)(2,1)S(1)} %slice.36), channel_id=1, source_target_pairs={{0,4},{1,5},{2,6},{3,7},{4,0},{5,1},{6,2},{7,3},{8,12},{9,13},{10,... | collective-permute-start | bytes 3932168 | tf_op jit(solution)/shard_map/ppermute | solution.py:210
  228.0 33.7 %collective-permute-start.12 = (bf16[512,1280]{1,0:T(8,128)(2,1)}, bf16[512,1280]{1,0:T(8,128)(2,1)}, u32[]{:S(2)}, u32[]{:S(2)}) collective-permute-start(bf16[512,1280]{1,0:T(8,128)(2,1)} %slice.37), channel_id=1, source_target_pairs={{0,2},{1,3},{2,0},{3,1},{4,6},{5,7},{6,4},{7,5},{8,10},{9,11},{10,... | collective-permute-start | bytes 3932168 | tf_op jit(solution)/shard_map/ppermute | solution.py:210
  237.2 38.6 %collective-permute-start.7 = (bf16[512,1280]{1,0:T(8,128)(2,1)}, bf16[512,1280]{1,0:T(8,128)(2,1)}, u32[]{:S(2)}, u32[]{:S(2)}) collective-permute-start(bf16[512,1280]{1,0:T(8,128)(2,1)} %collective-permute-done.2.refs_3_), channel_id=1, source_target_pairs={{0,1},{1,0},{2,3},{3,2},{4,5},{5,4},{6,7},{7,6},{8,9},{9,8},{10,11... | collective-permute-start | bytes 3932168 | tf_op jit(solution)/shard_map/ppermute | solution.py:210
  255.5 20.6 %collective-permute-start.8 = (bf16[512,1280]{1,0:T(8,128)(2,1)}, bf16[512,1280]{1,0:T(8,128)(2,1)}, u32[]{:S(2)}, u32[]{:S(2)}) collective-permute-start(bf16[512,1280]{1,0:T(8,128)(2,1)} %collective-permute-done.3.refs_4_), channel_id=1, source_target_pairs={{0,1},{1,0},{2,3},{3,2},{4,5},{5,4},{6,7},{7,6},{8,9},{9,8},{10,11... | collective-permute-start | bytes 3932168 | tf_op jit(solution)/shard_map/ppermute | solution.py:210
  261.7 50.2 %collective-permute-start.13 = (bf16[1024,1280]{1,0:T(8,128)(2,1)}, bf16[1024,1280]{1,0:T(8,128)(2,1)}, u32[]{:S(2)}, u32[]{:S(2)}) collective-permute-start(bf16[1024,1280]{1,0:T(8,128)(2,1)} %add_convert_fusion.refs_10_.refs_1_), channel_id=1, source_target_pairs={{0,1},{1,0},{2,3},{3,2},{4,5},{5,4},{6,7},{7,6},{8,9},{9,8},{10,11... | collective-permute-start | bytes 7864328 | tf_op jit(solution)/shard_map/ppermute | solution.py:210
  261.7 50.5 %collective-permute-start.14 = (bf16[1024,1280]{1,0:T(8,128)(2,1)}, bf16[1024,1280]{1,0:T(8,128)(2,1)}, u32[]{:S(2)}, u32[]{:S(2)}) collective-permute-start(bf16[1024,1280]{1,0:T(8,128)(2,1)} %collective-permute-done.9.refs_11_.refs_2_), channel_id=1, source_target_pairs={{0,1},{1,0},{2,3},{3,2},{4,5},{5,4},{6,7},{7,6},{8,9},{9,8},{10,11... | collective-permute-start | bytes 7864328 | tf_op jit(solution)/shard_map/ppermute | solution.py:210
  262.2 50.3 %collective-permute-start.15 = (bf16[1024,1280]{1,0:T(8,128)(2,1)}, bf16[1024,1280]{1,0:T(8,128)(2,1)}, u32[]{:S(2)}, u32[]{:S(2)}) collective-permute-start(bf16[1024,1280]{1,0:T(8,128)(2,1)} %collective-permute-done.10.refs_12_.refs_3_), channel_id=1, source_target_pairs={{0,1},{1,0},{2,3},{3,2},{4,5},{5,4},{6,7},{7,6},{8,9},{9,8},{10,11... | collective-permute-start | bytes 7864328 | tf_op jit(solution)/shard_map/ppermute | solution.py:210
  275.8 36.9 %collective-permute-start.16 = (bf16[512,1280]{1,0:T(8,128)(2,1)}, bf16[512,1280]{1,0:T(8,128)(2,1)}, u32[]{:S(2)}, u32[]{:S(2)}) collective-permute-start(bf16[512,1280]{1,0:T(8,128)(2,1)} %collective-permute-done.11.refs_13_.refs_4_), channel_id=1, source_target_pairs={{0,1},{1,0},{2,3},{3,2},{4,5},{5,4},{6,7},{7,6},{8,9},{9,8},{10,11... | collective-permute-start | bytes 3932168 | tf_op jit(solution)/shard_map/ppermute | solution.py:210
  276.1 36.9 %collective-permute-start.17 = (bf16[512,1280]{1,0:T(8,128)(2,1)}, bf16[512,1280]{1,0:T(8,128)(2,1)}, u32[]{:S(2)}, u32[]{:S(2)}) collective-permute-start(bf16[512,1280]{1,0:T(8,128)(2,1)} %collective-permute-done.12.refs_14_.refs_5_), channel_id=1, source_target_pairs={{0,1},{1,0},{2,3},{3,2},{4,5},{5,4},{6,7},{7,6},{8,9},{9,8},{10,11... | collective-permute-start | bytes 3932168 | tf_op jit(solution)/shard_map/ppermute | solution.py:210
  311.9 108.6 %collective-permute-start.28 = (bf16[1024,1280]{1,0:T(8,128)(2,1)}, bf16[1024,1280]{1,0:T(8,128)(2,1)}, u32[]{:S(2)}, u32[]{:S(2)}) collective-permute-start(bf16[1024,1280]{1,0:T(8,128)(2,1)} %add_convert_fusion.2.refs_0_), channel_id=1, source_target_pairs={{0,1},{1,0},{2,3},{3,2},{4,5},{5,4},{6,7},{7,6},{8,9},{9,8},{10,11... | collective-permute-start | bytes 7864328 | tf_op jit(solution)/shard_map/ppermute | solution.py:210
  312.3 133.5 %collective-permute-start.31 = (bf16[1024,1280]{1,0:T(8,128)(2,1)}, bf16[1024,1280]{1,0:T(8,128)(2,1)}, u32[]{:S(2)}, u32[]{:S(2)}) collective-permute-start(bf16[1024,1280]{1,0:T(8,128)(2,1)} %multiply_convert_fusion.refs_4_.refs_1_), channel_id=1, source_target_pairs={{0,1},{1,0},{2,3},{3,2},{4,5},{5,4},{6,7},{7,6},{8,9},{9,8},{10,11... | collective-permute-start | bytes 7864328 | tf_op jit(solution)/shard_map/ppermute | solution.py:210
  312.5 109.4 %collective-permute-start.29 = (bf16[1024,1280]{1,0:T(8,128)(2,1)}, bf16[1024,1280]{1,0:T(8,128)(2,1)}, u32[]{:S(2)}, u32[]{:S(2)}) collective-permute-start(bf16[1024,1280]{1,0:T(8,128)(2,1)} %collective-permute-done.27.refs_1_), channel_id=1, source_target_pairs={{0,1},{1,0},{2,3},{3,2},{4,5},{5,4},{6,7},{7,6},{8,9},{9,8},{10,11... | collective-permute-start | bytes 7864328 | tf_op jit(solution)/shard_map/ppermute | solution.py:210
  312.8 133.0 %collective-permute-start.32 = (bf16[1024,1280]{1,0:T(8,128)(2,1)}, bf16[1024,1280]{1,0:T(8,128)(2,1)}, u32[]{:S(2)}, u32[]{:S(2)}) collective-permute-start(bf16[1024,1280]{1,0:T(8,128)(2,1)} %collective-permute-done.30.refs_5_.refs_2_), channel_id=1, source_target_pairs={{0,1},{1,0},{2,3},{3,2},{4,5},{5,4},{6,7},{7,6},{8,9},{9,8},{10,11... | collective-permute-start | bytes 7864328 | tf_op jit(solution)/shard_map/ppermute | solution.py:210
  387.2 122.7 %collective-permute-start.18 = (f32[320,640]{1,0:T(8,128)S(1)}, f32[320,640]{1,0:T(8,128)}, u32[]{:S(2)}, u32[]{:S(2)}) collective-permute-start(f32[320,640]{1,0:T(8,128)S(1)} %get-tuple-element.32), channel_id=1, source_target_pairs={{0,8},{1,9},{2,10},{3,11},{4,12},{5,13},{6,14},{7,15}} | collective-permute-start | bytes 2457608 | tf_op jit(solution)/shard_map/ppermute | solution.py:210
  420.5 95.6 %collective-permute-start.38 = (f32[160,1280]{1,0:T(8,128)}, f32[160,1280]{1,0:T(8,128)}, u32[]{:S(2)}, u32[]{:S(2)}) collective-permute-start(f32[160,1280]{1,0:T(8,128)} %get-tuple-element.28), channel_id=1, source_target_pairs={{0,8},{1,9},{2,10},{3,11},{4,12},{5,13},{6,14},{7,15}} | collective-permute-start | bytes 2457608 | tf_op jit(solution)/shard_map/ppermute | solution.py:210
  505.2 73.4 %collective-permute-start.33 = (f32[2,2,2,2,40,1280]{5,4,3,2,1,0:T(8,128)}, f32[2,2,2,2,40,1280]{5,4,3,2,1,0:T(8,128)}, u32[]{:S(2)}, u32[]{:S(2)}) collective-permute-start(f32[2,2,2,2,40,1280]{5,4,3,2,1,0:T(8,128)} %dynamic-slice_bitcast_fusion.1), channel_id=1, source_target_pairs={{0,4},{1,5},{2,6},{3,7},{4,0},{5,1},{6,2},{7,3},{8,12},{9,13},{10,... | collective-permute-start | bytes 9830408 | tf_op jit(solution)/shard_map/ppermute | solution.py:210
  506.8 37.1 %collective-permute-start.21 = (f32[320,640]{1,0:T(8,128)S(1)}, f32[320,640]{1,0:T(8,128)}, u32[]{:S(2)}, u32[]{:S(2)}) collective-permute-start(f32[320,640]{1,0:T(8,128)S(1)} %get-tuple-element.33), channel_id=1, source_target_pairs={{24,16},{25,17},{26,18},{27,19},{28,20},{29,21},{30,22},{31,23}} | collective-permute-start | bytes 2457608 | tf_op jit(solution)/shard_map/ppermute | solution.py:210
  508.4 45.5 %collective-permute-start.41 = (f32[160,1280]{1,0:T(8,128)}, f32[160,1280]{1,0:T(8,128)}, u32[]{:S(2)}, u32[]{:S(2)}) collective-permute-start(f32[160,1280]{1,0:T(8,128)} %get-tuple-element.29), channel_id=1, source_target_pairs={{24,16},{25,17},{26,18},{27,19},{28,20},{29,21},{30,22},{31,23}} | collective-permute-start | bytes 2457608 | tf_op jit(solution)/shard_map/ppermute | solution.py:210
  512.3 31.7 %collective-permute-start.19 = (f32[320,640]{1,0:T(8,128)}, f32[320,640]{1,0:T(8,128)S(1)}, u32[]{:S(2)}, u32[]{:S(2)}) collective-permute-start(f32[320,640]{1,0:T(8,128)} %bitcast_add_fusion.13), channel_id=1, source_target_pairs={{0,8},{1,9},{2,10},{3,11},{4,12},{5,13},{6,14},{7,15},{8,16},{9,17... | collective-permute-start | bytes 2457608 | tf_op jit(solution)/shard_map/ppermute | solution.py:210
  518.5 40.2 %collective-permute-start.39 = (f32[160,1280]{1,0:T(8,128)}, f32[160,1280]{1,0:T(8,128)}, u32[]{:S(2)}, u32[]{:S(2)}) collective-permute-start(f32[160,1280]{1,0:T(8,128)} %bitcast_add_fusion.7), channel_id=1, source_target_pairs={{0,8},{1,9},{2,10},{3,11},{4,12},{5,13},{6,14},{7,15},{8,16},{9,17... | collective-permute-start | bytes 2457608 | tf_op jit(solution)/shard_map/ppermute | solution.py:210
  547.0 23.3 %collective-permute-start.22 = (f32[320,640]{1,0:T(8,128)}, f32[320,640]{1,0:T(8,128)}, u32[]{:S(2)}, u32[]{:S(2)}) collective-permute-start(f32[320,640]{1,0:T(8,128)} %get-tuple-element.31), channel_id=1, source_target_pairs={{16,8},{17,9},{18,10},{19,11},{20,12},{21,13},{22,14},{23,15},{24,... | collective-permute-start | bytes 2457608 | tf_op jit(solution)/shard_map/ppermute | solution.py:210
  548.3 10.5 %copy-start = (f32[640,1280]{1,0:T(8,128)S(1)}, f32[640,1280]{1,0:T(8,128)}, u32[]{:S(2)}) copy-start(f32[640,1280]{1,0:T(8,128)} %shard_map.63) | copy-start | bytes 9830404
  552.4 74.1 %collective-permute-start.44 = (f32[2,2,160,1280]{3,2,1,0:T(8,128)}, f32[2,2,160,1280]{3,2,1,0:T(8,128)}, u32[]{:S(2)}, u32[]{:S(2)}) collective-permute-start(f32[2,2,160,1280]{3,2,1,0:T(8,128)} %dynamic-slice_bitcast_fusion), channel_id=1, source_target_pairs={{0,2},{1,3},{2,0},{3,1},{4,6},{5,7},{6,4},{7,5},{8,10},{9,11},{10,... | collective-permute-start | bytes 9830408 | tf_op jit(solution)/shard_map/ppermute | solution.py:210
  553.9 18.6 %copy-start.1 = (f32[1280,640]{1,0:T(8,128)S(1)}, f32[1280,640]{1,0:T(8,128)}, u32[]{:S(2)}) copy-start(f32[1280,640]{1,0:T(8,128)} %shard_map.60) | copy-start | bytes 9830404
  553.9 34.3 %collective-permute-start.20 = (f32[320,640]{1,0:T(8,128)}, f32[320,640]{1,0:T(8,128)S(1)}, u32[]{:S(2)}, u32[]{:S(2)}) collective-permute-start(f32[320,640]{1,0:T(8,128)} %get-tuple-element.30), channel_id=1, source_target_pairs={{0,8},{1,9},{2,10},{3,11},{4,12},{5,13},{6,14},{7,15},{8,16},{9,17... | collective-permute-start | bytes 2457608 | tf_op jit(solution)/shard_map/ppermute | solution.py:210
  560.3 44.6 %collective-permute-start.42 = (f32[160,1280]{1,0:T(8,128)S(1)}, f32[160,1280]{1,0:T(8,128)S(1)}, u32[]{:S(2)}, u32[]{:S(2)}) collective-permute-start(f32[160,1280]{1,0:T(8,128)S(1)} %get-tuple-element.27), channel_id=1, source_target_pairs={{16,8},{17,9},{18,10},{19,11},{20,12},{21,13},{22,14},{23,15},{24,... | collective-permute-start | bytes 2457608 | tf_op jit(solution)/shard_map/ppermute | solution.py:210
  570.3 102.6 %collective-permute-start.40 = (f32[160,1280]{1,0:T(8,128)S(1)}, f32[160,1280]{1,0:T(8,128)S(1)}, u32[]{:S(2)}, u32[]{:S(2)}) collective-permute-start(f32[160,1280]{1,0:T(8,128)S(1)} %get-tuple-element.26), channel_id=1, source_target_pairs={{0,8},{1,9},{2,10},{3,11},{4,12},{5,13},{6,14},{7,15},{8,16},{9,17... | collective-permute-start | bytes 2457608 | tf_op jit(solution)/shard_map/ppermute | solution.py:210
  578.6 25.5 %collective-permute-start.23 = (f32[320,640]{1,0:T(8,128)S(1)}, f32[320,640]{1,0:T(8,128)S(1)}, u32[]{:S(2)}, u32[]{:S(2)}) collective-permute-start(f32[320,640]{1,0:T(8,128)S(1)} %bitcast_add_fusion.12), channel_id=1, source_target_pairs={{8,0},{9,1},{10,2},{11,3},{12,4},{13,5},{14,6},{15,7},{16,8},{17,9... | collective-permute-start | bytes 2457608 | tf_op jit(solution)/shard_map/ppermute | solution.py:210
  588.1 38.4 %slice-start = ((s8[6553600]{0:T(1024)(128)(4,1)}), s8[4194304]{0:T(1024)(128)(4,1)S(1)}, s32[]{:S(2)}) async-start(s8[6553600]{0:T(1024)(128)(4,1)} %bitcast.264), calls=%async_computation | async-start | bytes 8388608
  588.2 38.2 %slice-start.1 = ((s8[6553600]{0:T(1024)(128)(4,1)}), s8[2359296]{0:T(1024)(128)(4,1)S(1)}, s32[]{:S(2)}) async-start(s8[6553600]{0:T(1024)(128)(4,1)} %bitcast.264), calls=%async_computation.1 | async-start | bytes 4718592
  588.2 80.9 %collective-permute-start.34 = (f32[2,2,2,40,1280]{4,3,2,1,0:T(8,128)S(1)}, f32[2,2,2,40,1280]{4,3,2,1,0:T(8,128)S(1)}, u32[]{:S(2)}, u32[]{:S(2)}) collective-permute-start(f32[2,2,2,40,1280]{4,3,2,1,0:T(8,128)S(1)} %dynamic-slice_bitcast_fusion.3), channel_id=1, source_target_pairs={{0,2},{1,3},{2,0},{3,1},{4,6},{5,7},{6,4},{7,5},{8,10},{9,11},{10,... | collective-permute-start | bytes 4915208 | tf_op jit(solution)/shard_map/ppermute | solution.py:210
  604.3 10.5 %collective-permute-start.24 = (f32[2,2,40,640]{3,2,1,0:T(8,128)S(1)}, f32[2,2,40,640]{3,2,1,0:T(8,128)S(1)}, u32[]{:S(2)}, u32[]{:S(2)}) collective-permute-start(f32[2,2,40,640]{3,2,1,0:T(8,128)S(1)} %dynamic-slice_bitcast_fusion.23), channel_id=1, source_target_pairs={{0,4},{1,5},{2,6},{3,7},{4,0},{5,1},{6,2},{7,3},{8,12},{9,13},{10,... | collective-permute-start | bytes 1228808 | tf_op jit(solution)/shard_map/ppermute | solution.py:210
  605.0 67.9 %collective-permute-start.43 = (f32[160,1280]{1,0:T(8,128)S(1)}, f32[160,1280]{1,0:T(8,128)S(1)}, u32[]{:S(2)}, u32[]{:S(2)}) collective-permute-start(f32[160,1280]{1,0:T(8,128)S(1)} %bitcast_add_fusion.6), channel_id=1, source_target_pairs={{8,0},{9,1},{10,2},{11,3},{12,4},{13,5},{14,6},{15,7},{16,8},{17,9... | collective-permute-start | bytes 2457608 | tf_op jit(solution)/shard_map/ppermute | solution.py:210
  614.9 54.2 %collective-permute-start.25 = (f32[2,2,40,640]{3,2,0,1:T(8,128)S(1)}, f32[2,2,40,640]{3,2,0,1:T(8,128)S(1)}, u32[]{:S(2)}, u32[]{:S(2)}) collective-permute-start(f32[2,2,40,640]{3,2,0,1:T(8,128)S(1)} %fusion.87), channel_id=1, source_target_pairs={{0,2},{1,3},{2,0},{3,1},{4,6},{5,7},{6,4},{7,5},{8,10},{9,11},{10,... | collective-permute-start | bytes 1228808 | tf_op jit(solution)/shard_map/ppermute | solution.py:210
  628.9 81.1 %collective-permute-start.45 = (f32[2,160,1280]{2,1,0:T(8,128)S(1)}, f32[2,160,1280]{2,1,0:T(8,128)S(1)}, u32[]{:S(2)}, u32[]{:S(2)}) collective-permute-start(f32[2,160,1280]{2,1,0:T(8,128)S(1)} %dynamic-slice_bitcast_fusion.2), channel_id=1, source_target_pairs={{0,4},{1,5},{2,6},{3,7},{4,0},{5,1},{6,2},{7,3},{8,12},{9,13},{10,... | collective-permute-start | bytes 4915208 | tf_op jit(solution)/shard_map/ppermute | solution.py:210
  669.4 37.2 %collective-permute-start.35 = (f32[2,2,40,1280]{3,2,1,0:T(8,128)S(1)}, f32[2,2,40,1280]{3,2,1,0:T(8,128)S(1)}, u32[]{:S(2)}, u32[]{:S(2)}) collective-permute-start(f32[2,2,40,1280]{3,2,1,0:T(8,128)S(1)} %dynamic-slice_bitcast_fusion.7), channel_id=1, source_target_pairs={{0,16},{1,17},{2,18},{3,19},{4,20},{5,21},{6,22},{7,23},{8,24},{9,... | collective-permute-start | bytes 2457608 | tf_op jit(solution)/shard_map/ppermute | solution.py:210
  672.8 1.8 collective-permute-start.26
  706.8 3.3 copy-start.3
  707.6 18.9 %collective-permute-start.36 = (f32[2,40,1280]{2,1,0:T(8,128)}, f32[2,40,1280]{2,1,0:T(8,128)}, u32[]{:S(2)}, u32[]{:S(2)}) collective-permute-start(f32[2,40,1280]{2,1,0:T(8,128)} %dynamic-slice_bitcast_fusion.22), channel_id=1, source_target_pairs={{0,8},{1,9},{2,10},{3,11},{4,12},{5,13},{6,14},{7,15},{8,0},{9,1},... | collective-permute-start | bytes 1228808 | tf_op jit(solution)/shard_map/ppermute | solution.py:210
  711.3 36.7 %collective-permute-start.46 = (f32[160,1280]{1,0:T(8,128)}, f32[160,1280]{1,0:T(8,128)}, u32[]{:S(2)}, u32[]{:S(2)}) collective-permute-start(f32[160,1280]{1,0:T(8,128)} %dynamic-slice_bitcast_fusion.4), channel_id=1, source_target_pairs={{0,16},{1,17},{2,18},{3,19},{4,20},{5,21},{6,22},{7,23},{8,24},{9,... | collective-permute-start | bytes 2457608 | tf_op jit(solution)/shard_map/ppermute | solution.py:210
  717.2 32.0 %copy-start.2 = (f32[1,160,1280]{2,1,0:T(8,128)S(1)}, f32[1,160,1280]{2,1,0:T(8,128)}, u32[]{:S(2)}) copy-start(f32[1,160,1280]{2,1,0:T(8,128)} %fusion.76) | copy-start | bytes 2457604
  727.8 22.7 %collective-permute-start.37 = (f32[2,40,1280]{2,1,0:T(8,128)S(1)}, f32[2,40,1280]{2,1,0:T(8,128)S(1)}, u32[]{:S(2)}, u32[]{:S(2)}) collective-permute-start(f32[2,40,1280]{2,1,0:T(8,128)S(1)} %fusion.79), channel_id=1, source_target_pairs={{0,1},{1,0},{2,3},{3,2},{4,5},{5,4},{6,7},{7,6},{8,9},{9,8},{10,11... | collective-permute-start | bytes 1228808 | tf_op jit(solution)/shard_map/ppermute | solution.py:210
where the time goes:
time: 771 us; the launch traced here: 757 us
  waiting for transfers between devices  238 us (31%)
  Pallas kernels  230 us (30%)
  matrix products  135 us (18%)
  local copies, waits for them, and re-layouts  66.6 us (9%)
  starting transfers between devices  58.2 us (8%)
  other arithmetic  28.6 us (4%)
    ppermute x47, waiting for transfers between devices, permute(): return lax.ppermute(v, 'data', pairs)  238 us
    pallas_call x6, Pallas kernels, call(): pl.pallas_call(kernel, out_shape=out_shape, in_specs=in_specs, out_specs=...  230 us
    dot_general x6, matrix products, dot(): return lax.dot_general(a, b, (dims, ((), ())), preferred_element_type=F32)  135 us
    ppermute x47, starting transfers between devices, permute(): return lax.ppermute(v, 'data', pairs)  58.2 us
  transfers between devices with their start and end apart: 47, of which 15 were waited for; matrix products, arithmetic and copies ran while one was open for 29% of the time, Pallas kernels for 30%

commit v1 on v0

--- a/solution.py
+++ b/solution.py
@@ -10,6 +10,10 @@
 F32, BF16 = jnp.float32, jnp.bfloat16
 
 
+OUT_ROUTES = {"a": (4, (2, 4, 16)), "b": (3, (4, 2, 16)), "c": (3, (16, 2, 4))}
+IN_ROUTES = {"a": (5, (4, 2, 16)), "b": (5, (2, 4, 16))}
+
+
 def gelu_act(pre_f32):
     return jax.nn.gelu(pre_f32, approximate=True)
 
@@ -28,12 +32,12 @@
     return pullback(grad_act.astype(F32))[0].astype(BF16)
 
 
-def start_rows(refs, buf, sems, piece):
-    k = 0
-    for ref in refs:
-        for r in range(0, ref.shape[0], piece):
+def start_rows(*streams, piece):
+    todo = [[(ref, r, buf, sems) for ref in refs for r in range(0, ref.shape[0], piece)] for refs, buf, sems in streams]
+    for k in range(len(todo[0])):
+        for stream in todo:
+            ref, r, buf, sems = stream[k]
             pltpu.make_async_copy(ref.at[pl.ds(r, piece)], buf.at[pl.ds(k * piece, piece)], sems.at[k]).start()
-            k += 1
 
 
 def wait_rows(buf, sems, piece, tile, i):
@@ -47,9 +51,37 @@
     nbytes = sum(o.size * o.dtype.itemsize for o in operands)
     return pl.pallas_call(
         kernel, out_shape=out_shape, in_specs=in_specs, out_specs=out_specs, scratch_shapes=scratch,
-        compiler_params=pltpu.CompilerParams(vmem_limit_bytes=62 * 1024 * 1024),
+        compiler_params=pltpu.CompilerParams(vmem_limit_bytes=63 * 1024 * 1024),
         cost_estimate=pl.CostEstimate(flops=flops, bytes_accessed=nbytes, transcendentals=0),
     )(*operands)
+
+
+def accumulate(i, steps, n_parts, chunk, part_of, acc, out_ref, out_sems):
+    def part(c, _):
+        at = pl.ds(pl.multiple_of(c * chunk, chunk), chunk)
+        val = part_of(at)
+
+        @pl.when(i == 0)
+        def _():
+            acc[at, :] = val
+
+        @pl.when(i > 0)
+        def _():
+            acc[at, :] += val
+
+        @pl.when(i == steps - 1)
+        def _():
+            pltpu.make_async_copy(acc.at[at], out_ref.at[at], out_sems.at[c]).start()
+
+        return 0
+
+    lax.fori_loop(0, n_parts, part, 0)
+
+
+def finish(n_parts, chunk, acc, out_ref, out_sems):
+    for c in range(n_parts):
+        at = pl.ds(c * chunk, chunk)
+        pltpu.make_async_copy(acc.at[at], out_ref.at[at], out_sems.at[c]).wait()
 
 
 def sizes_of(blocks):
@@ -58,14 +90,27 @@
     return piece, total, blocks[0].shape[1]
 
 
-def share_forward(blocks, w):
+def share_forward(blocks, w_in, layer, owners_of, fr):
     piece, total, d = sizes_of(blocks)
-    cols = w.shape[1]
+    piece = min(piece, 512)
+    ff = w_in.shape[2]
+    count = len(owners_of(jnp.int32(0)))
+    cols, wide = count * fr, min(256, ff)
     nb, steps = len(blocks), total // piece
 
     def kernel(*refs):
-        h_refs, (w_ref, pre_ref, act_ref, h_buf, pre_buf, act_buf, sems, out_sems) = refs[:nb], refs[nb:]
-        start_rows(h_refs, h_buf, sems, piece)
+        h_refs, (w_ref, pre_ref, act_ref, h_buf, win, w_buf, pre_buf, act_buf, sems, w_sems, out_sems) = refs[:nb], refs[nb:]
+        owners = owners_of(lax.axis_index("data"))
+        starts = [jnp.minimum((o * fr) // 128 * 128, ff - wide) for o in owners]
+        for k, at in enumerate(starts):
+            pltpu.make_async_copy(w_ref.at[layer, :, pl.ds(pl.multiple_of(at, 128), wide)], win.at[k], w_sems.at[k]).start()
+        start_rows((h_refs, h_buf, sems), piece=piece)
+        row = lax.broadcasted_iota(jnp.int32, (wide, fr), 0)
+        col = lax.broadcasted_iota(jnp.int32, (wide, fr), 1)
+        for k, (o, at) in enumerate(zip(owners, starts)):
+            pltpu.make_async_copy(win.at[k], win.at[k], w_sems.at[k]).wait()
+            pick = jnp.where(row == col + (o * fr - at), 1.0, 0.0).astype(BF16)
+            w_buf[:, k * fr:(k + 1) * fr] = dot(win[k], pick, NN).astype(BF16)
 
         def outs(i, slot):
             rows = pl.ds(i * piece, piece)
@@ -81,7 +126,7 @@
                 for c in outs(i - 2, slot):
                     c.wait()
 
-            pre = dot(h_buf[pl.ds(i * piece, piece), :], w_ref[...], NN).astype(BF16)
+            pre = dot(h_buf[pl.ds(i * piece, piece), :], w_buf[...], NN).astype(BF16)
             pre_buf[slot] = pre
             act_buf[slot] = gelu_act(pre.astype(F32)).astype(BF16)
             for c in outs(i, slot):
@@ -94,74 +139,74 @@
                 c.wait()
 
     shape = jax.ShapeDtypeStruct((total, cols), BF16)
-    return call(kernel, [*blocks, w], [ANY] * nb + [WHOLE], [shape, shape], [ANY, ANY],
-                [pltpu.VMEM((total, d), BF16), pltpu.VMEM((2, piece, cols), BF16), pltpu.VMEM((2, piece, cols), BF16),
-                 pltpu.SemaphoreType.DMA((steps,)), pltpu.SemaphoreType.DMA((2, 2))], 2 * total * d * cols)
+    return call(kernel, [*blocks, w_in], [ANY] * (nb + 1), [shape, shape], [ANY, ANY],
+                [pltpu.VMEM((total, d), BF16), pltpu.VMEM((count, d, wide), BF16), pltpu.VMEM((d, cols), BF16),
+                 pltpu.VMEM((2, piece, cols), BF16), pltpu.VMEM((2, piece, cols), BF16),
+                 pltpu.SemaphoreType.DMA((steps,)), pltpu.SemaphoreType.DMA((count,)), pltpu.SemaphoreType.DMA((2, 2))],
+                2 * total * d * cols)
 
 
 def share_out(act, blocks):
     piece, total, d = sizes_of(blocks)
+    piece = min(piece, 512)
     cols = act.shape[1]
     nb, tile = len(blocks), 2 * piece
+    steps = total // tile
+    n_parts = 5 if cols % 640 == 0 else 1
+    chunk = cols // n_parts
 
     def kernel(*refs):
-        act_ref, g_refs, (out_ref, act_buf, g_buf, act_sems, sems) = refs[0], refs[1:1 + nb], refs[1 + nb:]
-        start_rows([act_ref], act_buf, act_sems, piece)
-        start_rows(g_refs, g_buf, sems, piece)
-        chunk = cols // 5 if cols % 640 == 0 else cols
+        act_ref, g_refs, (out_ref, act_buf, g_buf, acc, act_sems, sems, out_sems) = refs[0], refs[1:1 + nb], refs[1 + nb:]
+        start_rows(([act_ref], act_buf, act_sems), (g_refs, g_buf, sems), piece=piece)
 
         def step(i, _):
             wait_rows(act_buf, act_sems, piece, tile, i)
             wait_rows(g_buf, sems, piece, tile, i)
             rows = pl.ds(i * tile, tile)
-
-            def part(c, _):
-                at = pl.ds(pl.multiple_of(c * chunk, chunk), chunk)
-                val = dot(act_buf[rows, at], g_buf[rows, :], TN)
-
-                @pl.when(i == 0)
-                def _():
-                    out_ref[at, :] = val
-
-                @pl.when(i > 0)
-                def _():
-                    out_ref[at, :] += val
-
-                return 0
-
-            lax.fori_loop(0, cols // chunk, part, 0)
+            accumulate(i, steps, n_parts, chunk, lambda at: dot(act_buf[rows, at], g_buf[rows, :], TN), acc, out_ref, out_sems)
             return 0
 
-        lax.fori_loop(0, total // tile, step, 0)
-
-    return call(kernel, [act, *blocks], [ANY] * (nb + 1), jax.ShapeDtypeStruct((cols, d), F32), WHOLE,
-                [pltpu.VMEM((total, cols), BF16), pltpu.VMEM((total, d), BF16),
-                 pltpu.SemaphoreType.DMA((total // piece,)), pltpu.SemaphoreType.DMA((total // piece,))],
+        lax.fori_loop(0, steps, step, 0)
+        finish(n_parts, chunk, acc, out_ref, out_sems)
+
+    return call(kernel, [act, *blocks], [ANY] * (nb + 1), jax.ShapeDtypeStruct((cols, d), F32), ANY,
+                [pltpu.VMEM((total, cols), BF16), pltpu.VMEM((total, d), BF16), pltpu.VMEM((cols, d), F32),
+                 pltpu.SemaphoreType.DMA((total // piece,)), pltpu.SemaphoreType.DMA((total // piece,)),
+                 pltpu.SemaphoreType.DMA((n_parts,))],
                 2 * total * d * cols)
 
 
-def share_in(hs, gs, pre, w):
+def share_in(hs, gs, pre, w_out, layer, owners_of, fr):
     piece, total, d = sizes_of(hs)
-    cols = w.shape[0]
+    piece = min(piece, 512)
+    cols = pre.shape[1]
+    count = cols // fr
     nb, tile = len(hs), 2 * piece
     steps = total // tile
+    n_parts = 5 if d % 640 == 0 else 1
+    chunk = d // n_parts
 
     def kernel(*refs):
         h_refs, g_refs = refs[:nb], refs[nb:2 * nb]
-        pre_ref, w_ref, out_ref, h_buf, g_buf, pre_buf, v_buf, h_sems, g_sems, pre_sems = refs[2 * nb:]
-        start_rows(g_refs, g_buf, g_sems, piece)
-        start_rows(h_refs, h_buf, h_sems, piece)
+        (pre_ref, w_ref, out_ref, h_buf, g_buf, pre_buf, v_buf, w_buf, acc,
+         h_sems, g_sems, pre_sems, w_sems, out_sems) = refs[2 * nb:]
+        copies = [pltpu.make_async_copy(w_ref.at[layer, pl.ds(pl.multiple_of(o * fr, fr), fr)],
+                                        w_buf.at[pl.ds(k * fr, fr)], w_sems.at[k])
+                  for k, o in enumerate(owners_of(lax.axis_index("data")))]
+        for c in copies:
+            c.start()
 
         def fetch(i, slot):
             return pltpu.make_async_copy(pre_ref.at[pl.ds(i * tile, tile)], pre_buf.at[slot], pre_sems.at[slot])
 
         fetch(0, 0).start()
-        chunk = d // 5 if d % 640 == 0 else d
+        start_rows((g_refs, g_buf, g_sems), (h_refs, h_buf, h_sems), piece=piece)
+        for c in copies:
+            c.wait()
 
         def step(i, _):
             slot = i % 2
             wait_rows(g_buf, g_sems, piece, tile, i)
-            wait_rows(h_buf, h_sems, piece, tile, i)
             fetch(i, slot).wait()
 
             @pl.when(i + 1 < steps)
@@ -170,37 +215,26 @@
 
             def head(j, _):
                 sub = pl.ds(j * piece, piece)
-                e = dot(g_buf[pl.ds(i * tile + j * piece, piece), :], w_ref[...], NT).astype(BF16)
+                e = dot(g_buf[pl.ds(i * tile + j * piece, piece), :], w_buf[...], NT).astype(BF16)
                 v_buf[sub, :] = grad_pre_of(pre_buf[slot, sub, :], e)
                 return 0
 
             lax.fori_loop(0, 2, head, 0)
+            wait_rows(h_buf, h_sems, piece, tile, i)
             rows = pl.ds(i * tile, tile)
-
-            def part(c, _):
-                at = pl.ds(pl.multiple_of(c * chunk, chunk), chunk)
-                val = dot(h_buf[rows, at], v_buf[...], TN)
-
-                @pl.when(i == 0)
-                def _():
-                    out_ref[at, :] = val
-
-                @pl.when(i > 0)
-                def _():
-                    out_ref[at, :] += val
-
-                return 0
-
-            lax.fori_loop(0, d // chunk, part, 0)
+            accumulate(i, steps, n_parts, chunk, lambda at: dot(h_buf[rows, at], v_buf[...], TN), acc, out_ref, out_sems)
             return 0
 
         lax.fori_loop(0, steps, step, 0)
+        finish(n_parts, chunk, acc, out_ref, out_sems)
 
     n_sem = total // piece
-    return call(kernel, [*hs, *gs, pre, w], [ANY] * (2 * nb + 1) + [WHOLE], jax.ShapeDtypeStruct((d, cols), F32), WHOLE,
+    return call(kernel, [*hs, *gs, pre, w_out], [ANY] * (2 * nb + 2), jax.ShapeDtypeStruct((d, cols), F32), ANY,
                 [pltpu.VMEM((total, d), BF16), pltpu.VMEM((total, d), BF16), pltpu.VMEM((2, tile, cols), BF16),
-                 pltpu.VMEM((tile, cols), BF16), pltpu.SemaphoreType.DMA((n_sem,)), pltpu.SemaphoreType.DMA((n_sem,)),
-                 pltpu.SemaphoreType.DMA((2,))], 4 * total * d * cols)
+                 pltpu.VMEM((tile, cols), BF16), pltpu.VMEM((cols, d), BF16), pltpu.VMEM((d, cols), F32),
+                 pltpu.SemaphoreType.DMA((n_sem,)), pltpu.SemaphoreType.DMA((n_sem,)),
+                 pltpu.SemaphoreType.DMA((2,)), pltpu.SemaphoreType.DMA((count,)), pltpu.SemaphoreType.DMA((n_parts,))],
+                4 * total * d * cols)
 
 
 def solution(mesh):
@@ -263,14 +297,23 @@
             second = jnp.where(bit(b) == 0, recv, keep)
             return jnp.stack([first, second], axis=axis)
 
-        def share_of(w, layer, axis, owners):
-            start = lambda o: (layer, o * fr, 0) if axis == 0 else (layer, 0, o * fr)
-            size = (1, fr, d) if axis == 0 else (1, d, fr)
-            return jnp.concatenate([lax.dynamic_slice(w, start(o), size)[0] for o in owners], axis=axis)
-
-        owners1 = [(zh * 16 + y * 4 + x * 2) + bit(ZL) * 8 + bit(CORE)
-                   for zh in range(2) for y in range(2) for x in range(2)]
-        owners0 = [zz * 8 + idx % 8 for zz in range(4)]
+        def scatter(arr, names, routes):
+            width, at, parts = arr.shape[-1], 0, []
+            for (tenths, order) in routes.values():
+                size = width * tenths // 10
+                part, left = lax.slice_in_dim(arr, at, at + size, axis=arr.ndim - 1), list(names)
+                for b in order:
+                    part = halve(part, left.index(b), b)
+                    left.remove(b)
+                parts.append(part)
+                at += size
+            return jnp.concatenate(parts, axis=-1)
+
+        def owners1(i):
+            return [zh * 16 + y * 4 + x * 2 + (i // ZL) % 2 * 8 + i % 2 for zh in range(2) for y in range(2) for x in range(2)]
+
+        def owners0(i):
+            return [zz * 8 + i % 8 for zz in range(4)]
 
         h0s = plane_gather(tokens)
         pre0 = dot(tokens, w_in[0], NN).astype(BF16)
@@ -287,23 +330,16 @@
         g0 = (g1.astype(F32) + dot(grad_pre1, w_in[1], NT)).astype(BF16)
         g0s = plane_gather(g0)
 
-        w_in1, w_in0 = share_of(w_in, 1, 1, owners1), share_of(w_in, 0, 1, owners0)
-        w_out1, w_out0 = share_of(w_out, 1, 0, owners1), share_of(w_out, 0, 0, owners0)
-        pre1s, act1s = share_forward(h1s, w_in1)
-        pre0s, act0s = share_forward(h0s, w_in0)
+        pre1s, act1s = share_forward(h1s, w_in, 1, owners1, fr)
+        pre0s, act0s = share_forward(h0s, w_in, 0, owners0, fr)
         out1 = share_out(act1s, g1s)
-        in1 = share_in(h1s, g1s, pre1s, w_out1)
-        in0 = share_in(h0s, g0s, pre0s, w_out0)
+        in1 = share_in(h1s, g1s, pre1s, w_out, 1, owners1, fr)
         out0 = share_out(act0s, g0s)
-
-        out1 = out1.reshape(2, 2, 2, fr, d)
-        out1 = halve(out1, 2, X)
-        out1 = halve(out1, 1, Y)
-        out1 = halve(out1, 0, ZH)
+        in0 = share_in(h0s, g0s, pre0s, w_out, 0, owners0, fr)
+
+        out1 = scatter(out1.reshape(2, 2, 2, fr, d), [ZH, Y, X], OUT_ROUTES)
         in1 = in1.reshape(2, 2, 2, 2, 2, dr, 8 * fr)
-        in1 = halve(in1, 2, Y)
-        in1 = halve(in1, 2, X)
-        in1 = halve(in1, 0, ZH)
+        in1 = scatter(in1, [ZH, None, Y, X], IN_ROUTES)
         in1 = spread(spread(in1, 0, ZL), 1, CORE)
         in1 = in1.reshape(2, 2, dr, 2, 2, 2, fr)
         in1 = in1.transpose(2, 3, 0, 4, 5, 1, 6).reshape(dr, ff)

time: 771 us -> 799 us (1.036)
  waiting for transfers between devices: 238 us -> 285 us
  local copies, waits for them, and re-layouts: 66.6 us -> 32.6 us
  starting transfers between devices: 58.2 us -> 76 us
  other arithmetic: 28.6 us -> 13.3 us
    ppermute x47 -> x56, waiting for transfers between devices: 238 us -> 285 us  [permute(): return lax.ppermute(v, 'data', pairs)]
    ppermute x47 -> x56, starting transfers between devices: 58.2 us -> 76 us  [permute(): return lax.ppermute(v, 'data', pairs)]
    squeeze x2 -> x0, local copies, waits for them, and re-layouts: 11.4 us -> none  [share_of(): lax.dynamic_slice(w, start(o), size)[0]]
    concatenate x2 -> x0, local copies, waits for them, and re-layouts: 9.59 us -> none  [share_of(): jnp.concatenate([lax.dynamic_slice(w, start(o), size)[0] for o in owners]...]
    unnamed x23 -> x34, local copies, waits for them, and re-layouts: 12.5 us -> 3.18 us
  transfers between devices with their start and end apart: 47 -> 56, of which waited for: 15 -> 19; matrix products, arithmetic and copies ran while one was open for 29% -> 17% of each run, Pallas kernels for 30% -> 30%
where the time goes in v1:
time: 799 us; the launch traced here: 786 us
  waiting for transfers between devices  285 us (36%)
  Pallas kernels  237 us (30%)
  matrix products  141 us (18%)
  starting transfers between devices  76 us (10%)
  local copies, waits for them, and re-layouts  32.6 us (4%)
  other arithmetic  13.3 us (2%)
    ppermute x56, waiting for transfers between devices, permute(): return lax.ppermute(v, 'data', pairs)  285 us
    pallas_call x6, Pallas kernels, call(): pl.pallas_call(kernel, out_shape=out_shape, in_specs=in_specs, out_specs=...  237 us
    dot_general x6, matrix products, dot(): return lax.dot_general(a, b, (dims, ((), ())), preferred_element_type=F32)  141 us
    ppermute x56, starting transfers between devices, permute(): return lax.ppermute(v, 'data', pairs)  76 us
  transfers between devices with their start and end apart: 56, of which 19 were waited for; matrix products, arithmetic and copies ran while one was open for 17% of the time, Pallas kernels for 30%

profile of v1, /device:TPU:14, one launch (start us, length us, event | category | flops | bytes accessed | tf_op | source)
XLA Modules:
  0.0 786.4 jit_solution(15974046573351659340)
XLA Ops:
  0.6 22.7 %fusion.144 = bf16[1024,5120]{1,0:T(8,128)(2,1)} fusion(bf16[1024,1280]{1,0:T(8,128)(2,1)} %refs_0_.3, bf16[2,1280,5120]{2,1,0:T(8,128)(2,1)} %refs_4_.1), kind=kOutput, calls=%fused_computation.20.clone.clone.clone.clone.2 | convolution fusion | flops 13479444480 | bytes 26214400 | tf_op jit(solution)/shard_map/dot_general | solution.py:22
  23.3 20.9 %add_convert_fusion.2.refs_0_ = bf16[1024,1280]{1,0:T(8,128)(2,1)} fusion(bf16[1024,1280]{1,0:T(8,128)(2,1)S(1)} %copy-done.10, bf16[2,5120,1280]{2,1,0:T(8,128)(2,1)} %refs_9_.1, bf16[1024,5120]{1,0:T(8,128)(2,1)} %fusion.144), kind=kOutput, calls=%fused_computation.56 | convolution fusion | flops 13425704960 | bytes 28835840 | tf_op jit(solution)/shard_map/dot_general | solution.py:22
  44.7 20.3 %fusion.49 = bf16[1024,5120]{1,0:T(8,128)(2,1)} fusion(bf16[1024,1280]{1,0:T(8,128)(2,1)} %add_convert_fusion.2.refs_0_, bf16[2,1280,5120]{2,1,0:T(8,128)(2,1)} %refs_4_.1), kind=kOutput, calls=%fused_computation.52 | convolution fusion | flops 13427015680 | bytes 26214400 | tf_op jit(solution)/shard_map/dot_general | solution.py:22
  65.0 26.2 %multiply_convert_fusion.refs_4_.refs_1_ = bf16[1024,1280]{1,0:T(8,128)(2,1)} fusion(bf16[1024,1280]{1,0:T(8,128)(2,1)S(1)} %copy-done.9, bf16[2,5120,1280]{2,1,0:T(8,128)(2,1)} %refs_9_.1, bf16[1024,5120]{1,0:T(8,128)(2,1)} %fusion.49, bf16[1024,1280]{1,0:T(8,128)(2,1)} %add_convert_fusion.2.refs_0_), kind=kOutput, calls=%fused_computation.54 | convolution fusion | flops 13484687360 | bytes 31457280 | tf_op jit(solution)/shard_map/dot_general | solution.py:22
  91.2 1.5 collective-permute-start.30
  93.4 29.8 %fusion.140 = bf16[1024,5120]{1,0:T(8,128)(2,1)} fusion(bf16[1024,5120]{1,0:T(8,128)(2,1)} %fusion.49, bf16[1024,1280]{1,0:T(8,128)(2,1)} %multiply_convert_fusion.refs_4_.refs_1_, bf16[2,5120,1280]{2,1,0:T(8,128)(2,1)} %refs_9_.1), kind=kOutput, calls=%fused_computation.13.clone.clone.clone.clone.2 | convolution fusion | flops 13542359040 | bytes 36700160 | tf_op jit(solution)/shard_map/dot_general | solution.py:22
  123.7 1.3 collective-permute-start.4
  125.0 21.2 %add_convert_fusion.refs_10_.refs_1_ = bf16[1024,1280]{1,0:T(8,128)(2,1)} fusion(bf16[1024,1280]{1,0:T(8,128)(2,1)S(1)} %copy-done.12, bf16[2,1280,5120]{2,1,0:T(8,128)(2,1)} %refs_4_.1, bf16[1024,5120]{1,0:T(8,128)(2,1)} %fusion.140), kind=kOutput, calls=%fused_computation.53 | convolution fusion | flops 13425704960 | bytes 28835840 | tf_op jit(solution)/shard_map/dot_general | solution.py:22
  146.2 13.1 %collective-permute-done.30.refs_5_.refs_2_ = bf16[1024,1280]{1,0:T(8,128)(2,1)} collective-permute-done((bf16[1024,1280]{1,0:T(8,128)(2,1)}, bf16[1024,1280]{1,0:T(8,128)(2,1)}, u32[]{:S(2)}, u32[]{:S(2)}) %collective-permute-start.30) | collective-permute-done | bytes 2621472 | tf_op jit(solution)/shard_map/ppermute | solution.py:244
  160.4 1.8 slice.54
  162.2 20.2 %collective-permute-done.1.refs_2_ = bf16[1024,1280]{1,0:T(8,128)(2,1)} collective-permute-done((bf16[1024,1280]{1,0:T(8,128)(2,1)S(1)}, bf16[1024,1280]{1,0:T(8,128)(2,1)}, u32[]{:S(2)}, u32[]{:S(2)}) %collective-permute-start.1) | collective-permute-done | bytes 2621472 | tf_op jit(solution)/shard_map/ppermute | solution.py:244
  182.9 1.4 slice.55
  184.4 2.2 collective-permute-start.3
  186.5 32.8 %collective-permute-done.9.refs_11_.refs_2_ = bf16[1024,1280]{1,0:T(8,128)(2,1)S(1)} collective-permute-done((bf16[1024,1280]{1,0:T(8,128)(2,1)}, bf16[1024,1280]{1,0:T(8,128)(2,1)S(1)}, u32[]{:S(2)}, u32[]{:S(2)}) %collective-permute-start.9) | collective-permute-done | bytes 2621472 | tf_op jit(solution)/shard_map/ppermute | solution.py:244
  219.3 19.2 %collective-permute-done.10.refs_12_.refs_3_ = bf16[1024,1280]{1,0:T(8,128)(2,1)S(1)} collective-permute-done((bf16[1024,1280]{1,0:T(8,128)(2,1)}, bf16[1024,1280]{1,0:T(8,128)(2,1)S(1)}, u32[]{:S(2)}, u32[]{:S(2)}) %collective-permute-start.10) | collective-permute-done | bytes 2621472 | tf_op jit(solution)/shard_map/ppermute | solution.py:244
  238.5 1.3 collective-permute-start.5
  239.8 26.7 %collective-permute-done.2.refs_3_ = bf16[512,1280]{1,0:T(8,128)(2,1)S(1)} collective-permute-done((bf16[512,1280]{1,0:T(8,128)(2,1)S(1)}, bf16[512,1280]{1,0:T(8,128)(2,1)S(1)}, u32[]{:S(2)}, u32[]{:S(2)}) %collective-permute-start.2) | collective-permute-done | bytes 1310752 | tf_op jit(solution)/shard_map/ppermute | solution.py:244
  269.9 1.5 copy-done.14
  272.2 27.0 %shard_map.61 = (bf16[4096,1280]{1,0:T(8,128)(2,1)}, bf16[4096,1280]{1,0:T(8,128)(2,1)}) custom-call(bf16[1024,1280]{1,0:T(8,128)(2,1)} %add_convert_fusion.2.refs_0_, bf16[1024,1280]{1,0:T(8,128)(2,1)} %collective-permute-done.27.refs_1_, bf16[1024,1280]{1,0:T(8,128)(2,1)} %collective-permute-done.28.refs_2_, bf16[1024,1280]{1,0:T(8,128)(2,1)} %copy-done.14, ...), custom_call_target="tpu_custom_call" | custom-call | flops 13421772800 | bytes 36700160 | tf_op jit(solution)/shard_map/pallas_call | solution.py:52
  299.1 1.5 collective-permute-done.11.refs_13_.refs_4_
  300.6 1.8 collective-permute-done.12.refs_14_.refs_5_
  303.4 55.5 %shard_map.62 = f32[1280,1280]{1,0:T(8,128)} custom-call(bf16[1024,1280]{1,0:T(8,128)(2,1)} %add_convert_fusion.2.refs_0_, bf16[1024,1280]{1,0:T(8,128)(2,1)} %collective-permute-done.27.refs_1_, bf16[1024,1280]{1,0:T(8,128)(2,1)} %collective-permute-done.28.refs_2_, bf16[1024,1280]{1,0:T(8,128)(2,1)} %copy-done.14, ...), custom_call_target="tpu_custom_call" | custom-call | flops 26843545600 | bytes 57671680 | tf_op jit(solution)/shard_map/pallas_call | solution.py:52
  358.9 3.4 fusion.110
  362.3 1.6 copy-done.2
  364.0 1.6 dynamic-slice_bitcast_fusion.1
  367.4 31.8 %shard_map.59 = (bf16[8192,640]{1,0:T(8,128)(2,1)}, bf16[8192,640]{1,0:T(8,128)(2,1)}) custom-call(bf16[1024,1280]{1,0:T(8,128)(2,1)} %refs_0_.3, bf16[1024,1280]{1,0:T(8,128)(2,1)} %collective-permute-done.refs_1_, bf16[1024,1280]{1,0:T(8,128)(2,1)} %collective-permute-done.1.refs_2_, bf16[512,1280]{1,0:T(8,128)(2,1)} %copy-done.15, ...), custom_call_target="tpu_custom_call" | custom-call | flops 13421772800 | bytes 47185920 | tf_op jit(solution)/shard_map/pallas_call | solution.py:52
  399.3 1.5 collective-permute-start.33
  401.8 70.4 %shard_map.60 = f32[1280,640]{1,0:T(8,128)} custom-call(bf16[1024,1280]{1,0:T(8,128)(2,1)} %refs_0_.3, bf16[1024,1280]{1,0:T(8,128)(2,1)} %collective-permute-done.refs_1_, bf16[1024,1280]{1,0:T(8,128)(2,1)} %collective-permute-done.1.refs_2_, bf16[512,1280]{1,0:T(8,128)(2,1)} %copy-done.15, bf16[512,1280]{1,0:T(8,128)(2,1)} %copy-done.16, ...), custom_call_target="tpu_custom_call" | custom-call | flops 26843545600 | bytes 78643200 | tf_op jit(solution)/shard_map/pallas_call | solution.py:52
  472.2 2.7 dynamic-slice_bitcast_fusion.10
  474.9 1.3 collective-permute-start.18
  476.2 28.1 %shard_map.63 = f32[640,1280]{1,0:T(8,128)} custom-call(bf16[8192,640]{1,0:T(8,128)(2,1)} %get-tuple-element.8.refs_0_, bf16[1024,1280]{1,0:T(8,128)(2,1)} %add_convert_fusion.refs_10_.refs_1_, bf16[1024,1280]{1,0:T(8,128)(2,1)} %copy-done.7, bf16[1024,1280]{1,0:T(8,128)(2,1)} %copy-done.8, bf16[512,1280]{1,0:T(8,128)(2,1)} %collective-permute-done.11.refs_13_.refs_4_, ...), custom_call_target="tpu_custom_call" | custom-call | flops 13421772800 | bytes 31457280 | tf_op jit(solution)/shard_map/pallas_call | solution.py:52
  504.3 2.4 dynamic-slice_bitcast_fusion.6
  508.0 23.9 %shard_map.64 = f32[1280,1280]{1,0:T(8,128)} custom-call(bf16[4096,1280]{1,0:T(8,128)(2,1)} %get-tuple-element.9.refs_0_, bf16[1024,1280]{1,0:T(8,128)(2,1)} %multiply_convert_fusion.refs_4_.refs_1_, bf16[1024,1280]{1,0:T(8,128)(2,1)} %collective-permute-done.30.refs_5_.refs_2_, bf16[1024,1280]{1,0:T(8,128)(2,1)} %copy-done.13, ...), custom_call_target="tpu_custom_call" | custom-call | flops 13421772800 | bytes 20971520 | tf_op jit(solution)/shard_map/pallas_call | solution.py:52
  531.9 2.4 fusion.109
  534.4 3.2 collective-permute-start.53
  537.7 2.1 slice.60
  542.8 1.3 bitcast_add_fusion.7
  544.1 35.2 %collective-permute-done.53 = f32[2,2,160,384]{3,2,1,0:T(8,128)S(1)} collective-permute-done((f32[2,2,160,384]{3,2,1,0:T(8,128)S(1)}, f32[2,2,160,384]{3,2,1,0:T(8,128)S(1)}, u32[]{:S(2)}, u32[]{:S(2)}) %collective-permute-start.53) | collective-permute-done | bytes 983072 | tf_op jit(solution)/shard_map/ppermute | solution.py:244
  582.9 11.5 %collective-permute-done.54 = f32[2,160,384]{2,1,0:T(8,128)S(1)} collective-permute-done((f32[2,160,384]{2,1,0:T(8,128)S(1)}, f32[2,160,384]{2,1,0:T(8,128)S(1)}, u32[]{:S(2)}, u32[]{:S(2)}) %collective-permute-start.54) | collective-permute-done | bytes 491552 | tf_op jit(solution)/shard_map/ppermute | solution.py:244
  595.3 7.9 %collective-permute-done.51 = f32[2,160,384]{2,1,0:T(8,128)S(1)} collective-permute-done((f32[2,160,384]{2,1,0:T(8,128)S(1)}, f32[2,160,384]{2,1,0:T(8,128)S(1)}, u32[]{:S(2)}, u32[]{:S(2)}) %collective-permute-start.51) | collective-permute-done | bytes 491552 | tf_op jit(solution)/shard_map/ppermute | solution.py:244
  603.2 3.5 collective-permute-start.19
  606.9 2.2 collective-permute-start.42
  609.1 1.7 bitcast_add_fusion.1
  611.5 1.6 bitcast_add_fusion
  613.1 1.5 collective-permute-start.55
  614.6 12.0 %collective-permute-done.19 = f32[320,640]{1,0:T(8,128)S(1)} collective-permute-done((f32[320,640]{1,0:T(8,128)S(1)}, f32[320,640]{1,0:T(8,128)S(1)}, u32[]{:S(2)}, u32[]{:S(2)}) %collective-permute-start.19) | collective-permute-done | bytes 819232 | tf_op jit(solution)/shard_map/ppermute | solution.py:244
  627.8 23.9 %collective-permute-done.42 = f32[160,1280]{1,0:T(8,128)S(1)} collective-permute-done((f32[160,1280]{1,0:T(8,128)S(1)}, f32[160,1280]{1,0:T(8,128)S(1)}, u32[]{:S(2)}, u32[]{:S(2)}) %collective-permute-start.42) | collective-permute-done | bytes 819232 | tf_op jit(solution)/shard_map/ppermute | solution.py:244
  652.4 1.3 collective-permute-start.22
  653.8 4.8 collective-permute-start.49
  658.7 1.9 collective-permute-start.20
  660.7 14.9 %collective-permute-done.49 = f32[160,512]{1,0:T(8,128)S(1)} collective-permute-done((f32[160,512]{1,0:T(8,128)S(1)}, f32[160,512]{1,0:T(8,128)S(1)}, u32[]{:S(2)}, u32[]{:S(2)}) %collective-permute-start.49) | collective-permute-done | bytes 327712 | tf_op jit(solution)/shard_map/ppermute | solution.py:244
  675.6 1.3 collective-permute-start.45
  677.0 19.7 %collective-permute-start.43 = (f32[160,1280]{1,0:T(8,128)S(1)}, f32[160,1280]{1,0:T(8,128)S(1)}, u32[]{:S(2)}, u32[]{:S(2)}) collective-permute-start(f32[160,1280]{1,0:T(8,128)S(1)} %get-tuple-element.14), channel_id=1, source_target_pairs={{0,8},{1,9},{2,10},{3,11},{4,12},{5,13},{6,14},{7,15},{8,16},{9,17... | collective-permute-start | bytes 2457608 | tf_op jit(solution)/shard_map/ppermute | solution.py:244
  698.0 2.1 collective-permute-start.38
  700.2 31.3 %collective-permute-done.35 = f32[2,2,40,640]{3,2,1,0:T(8,128)S(1)} collective-permute-done((f32[2,2,40,640]{3,2,1,0:T(8,128)S(1)}, f32[2,2,40,640]{3,2,1,0:T(8,128)S(1)}, u32[]{:S(2)}, u32[]{:S(2)}) %collective-permute-start.35) | collective-permute-done | bytes 409632 | tf_op jit(solution)/shard_map/ppermute | solution.py:244
  731.5 1.9 collective-permute-start.23
  733.5 2.5 collective-permute-done.38
  736.6 3.5 collective-permute-start.46
  740.2 14.4 %collective-permute-done.23 = f32[320,640]{1,0:T(8,128)S(1)} collective-permute-done((f32[320,640]{1,0:T(8,128)S(1)}, f32[320,640]{1,0:T(8,128)S(1)}, u32[]{:S(2)}, u32[]{:S(2)}) %collective-permute-start.23) | collective-permute-done | bytes 819232 | tf_op jit(solution)/shard_map/ppermute | solution.py:244
  755.7 5.1 collective-permute-done.39
  761.0 1.7 collective-permute-done.24
  763.9 9.4 %collective-permute-done.46 = f32[160,1280]{1,0:T(8,128)S(1)} collective-permute-done((f32[160,1280]{1,0:T(8,128)S(1)}, f32[160,1280]{1,0:T(8,128)S(1)}, u32[]{:S(2)}, u32[]{:S(2)}) %collective-permute-start.46) | collective-permute-done | bytes 819232 | tf_op jit(solution)/shard_map/ppermute | solution.py:244
  779.3 1.8 stack_reshape.7
  784.7 1.3 pad_maximum_fusion
  (163 shorter events, 37.3 us)
Async XLA Ops:
  0.6 22.7 %copy-start.10 = (bf16[1024,1280]{1,0:T(8,128)(2,1)S(1)}, bf16[1024,1280]{1,0:T(8,128)(2,1)}, u32[]{:S(2)}) copy-start(bf16[1024,1280]{1,0:T(8,128)(2,1)} %refs_0_.3) | copy-start | bytes 7864324
  44.2 78.9 %collective-permute-start.27 = (bf16[1024,1280]{1,0:T(8,128)(2,1)}, bf16[1024,1280]{1,0:T(8,128)(2,1)}, u32[]{:S(2)}, u32[]{:S(2)}) collective-permute-start(bf16[1024,1280]{1,0:T(8,128)(2,1)} %add_convert_fusion.2.refs_0_), channel_id=1, source_target_pairs={{0,8},{1,9},{2,10},{3,11},{4,12},{5,13},{6,14},{7,15},{8,0},{9,1},... | collective-permute-start | bytes 7864328 | tf_op jit(solution)/shard_map/ppermute | solution.py:244
  44.7 79.0 %collective-permute-start.28 = (bf16[1024,1280]{1,0:T(8,128)(2,1)}, bf16[1024,1280]{1,0:T(8,128)(2,1)}, u32[]{:S(2)}, u32[]{:S(2)}) collective-permute-start(bf16[1024,1280]{1,0:T(8,128)(2,1)} %add_convert_fusion.2.refs_0_), channel_id=1, source_target_pairs={{0,1},{1,0},{2,3},{3,2},{4,5},{5,4},{6,7},{7,6},{8,9},{9,8},{10,11... | collective-permute-start | bytes 7864328 | tf_op jit(solution)/shard_map/ppermute | solution.py:244
  91.2 32.0 %copy-start.11 = (bf16[1024,1280]{1,0:T(8,128)(2,1)S(1)}, bf16[1024,1280]{1,0:T(8,128)(2,1)}, u32[]{:S(2)}) copy-start(bf16[1024,1280]{1,0:T(8,128)(2,1)} %refs_0_.3) | copy-start | bytes 7864324
  91.2 33.9 %copy-start.12 = (bf16[1024,1280]{1,0:T(8,128)(2,1)S(1)}, bf16[1024,1280]{1,0:T(8,128)(2,1)}, u32[]{:S(2)}) copy-start(bf16[1024,1280]{1,0:T(8,128)(2,1)} %multiply_convert_fusion.refs_4_.refs_1_) | copy-start | bytes 7864324
  91.2 68.2 %collective-permute-start.30 = (bf16[1024,1280]{1,0:T(8,128)(2,1)}, bf16[1024,1280]{1,0:T(8,128)(2,1)}, u32[]{:S(2)}, u32[]{:S(2)}) collective-permute-start(bf16[1024,1280]{1,0:T(8,128)(2,1)} %multiply_convert_fusion.refs_4_.refs_1_), channel_id=1, source_target_pairs={{0,8},{1,9},{2,10},{3,11},{4,12},{5,13},{6,14},{7,15},{8,0},{9,1},... | collective-permute-start | bytes 7864328 | tf_op jit(solution)/shard_map/ppermute | solution.py:244
  92.6 67.3 %collective-permute-start.31 = (bf16[1024,1280]{1,0:T(8,128)(2,1)}, bf16[1024,1280]{1,0:T(8,128)(2,1)S(1)}, u32[]{:S(2)}, u32[]{:S(2)}) collective-permute-start(bf16[1024,1280]{1,0:T(8,128)(2,1)} %multiply_convert_fusion.refs_4_.refs_1_), channel_id=1, source_target_pairs={{0,1},{1,0},{2,3},{3,2},{4,5},{5,4},{6,7},{7,6},{8,9},{9,8},{10,11... | collective-permute-start | bytes 7864328 | tf_op jit(solution)/shard_map/ppermute | solution.py:244
  92.8 67.6 %collective-permute-start = (bf16[1024,1280]{1,0:T(8,128)(2,1)}, bf16[1024,1280]{1,0:T(8,128)(2,1)}, u32[]{:S(2)}, u32[]{:S(2)}) collective-permute-start(bf16[1024,1280]{1,0:T(8,128)(2,1)} %refs_0_.3), channel_id=1, source_target_pairs={{0,2},{1,3},{2,0},{3,1},{4,6},{5,7},{6,4},{7,5},{8,10},{9,11},{10,... | collective-permute-start | bytes 7864328 | tf_op jit(solution)/shard_map/ppermute | solution.py:244
  123.1 59.3 %collective-permute-start.1 = (bf16[1024,1280]{1,0:T(8,128)(2,1)S(1)}, bf16[1024,1280]{1,0:T(8,128)(2,1)}, u32[]{:S(2)}, u32[]{:S(2)}) collective-permute-start(bf16[1024,1280]{1,0:T(8,128)(2,1)S(1)} %copy-done.11), channel_id=1, source_target_pairs={{0,4},{1,5},{2,6},{3,7},{4,0},{5,1},{6,2},{7,3},{8,12},{9,13},{10,... | collective-permute-start | bytes 7864328 | tf_op jit(solution)/shard_map/ppermute | solution.py:244
  123.7 60.6 %collective-permute-start.4 = (bf16[1024,1280]{1,0:T(8,128)(2,1)S(1)}, bf16[1024,1280]{1,0:T(8,128)(2,1)}, u32[]{:S(2)}, u32[]{:S(2)}) collective-permute-start(bf16[1024,1280]{1,0:T(8,128)(2,1)S(1)} %copy-done.11), channel_id=1, source_target_pairs={{0,1},{1,0},{2,3},{3,2},{4,5},{5,4},{6,7},{7,6},{8,9},{9,8},{10,11... | collective-permute-start | bytes 7864328 | tf_op jit(solution)/shard_map/ppermute | solution.py:244
  159.4 59.9 %collective-permute-start.9 = (bf16[1024,1280]{1,0:T(8,128)(2,1)}, bf16[1024,1280]{1,0:T(8,128)(2,1)S(1)}, u32[]{:S(2)}, u32[]{:S(2)}) collective-permute-start(bf16[1024,1280]{1,0:T(8,128)(2,1)} %add_convert_fusion.refs_10_.refs_1_), channel_id=1, source_target_pairs={{0,2},{1,3},{2,0},{3,1},{4,6},{5,7},{6,4},{7,5},{8,10},{9,11},{10,... | collective-permute-start | bytes 7864328 | tf_op jit(solution)/shard_map/ppermute | solution.py:244
  159.9 112.3 %copy-start.13 = (bf16[1024,1280]{1,0:T(8,128)(2,1)}, bf16[1024,1280]{1,0:T(8,128)(2,1)S(1)}, u32[]{:S(2)}) copy-start(bf16[1024,1280]{1,0:T(8,128)(2,1)S(1)} %collective-permute-done.31.refs_6_.refs_3_) | copy-start | bytes 7864324
  159.9 78.6 %collective-permute-start.10 = (bf16[1024,1280]{1,0:T(8,128)(2,1)}, bf16[1024,1280]{1,0:T(8,128)(2,1)S(1)}, u32[]{:S(2)}, u32[]{:S(2)}) collective-permute-start(bf16[1024,1280]{1,0:T(8,128)(2,1)} %add_convert_fusion.refs_10_.refs_1_), channel_id=1, source_target_pairs={{0,4},{1,5},{2,6},{3,7},{4,0},{5,1},{6,2},{7,3},{8,12},{9,13},{10,... | collective-permute-start | bytes 7864328 | tf_op jit(solution)/shard_map/ppermute | solution.py:244
  160.4 109.5 %collective-permute-start.29 = (bf16[1024,1280]{1,0:T(8,128)(2,1)}, bf16[1024,1280]{1,0:T(8,128)(2,1)S(1)}, u32[]{:S(2)}, u32[]{:S(2)}) collective-permute-start(bf16[1024,1280]{1,0:T(8,128)(2,1)} %collective-permute-done.27.refs_1_), channel_id=1, source_target_pairs={{0,1},{1,0},{2,3},{3,2},{4,5},{5,4},{6,7},{7,6},{8,9},{9,8},{10,11... | collective-permute-start | bytes 7864328 | tf_op jit(solution)/shard_map/ppermute | solution.py:244
  182.4 84.2 %collective-permute-start.2 = (bf16[512,1280]{1,0:T(8,128)(2,1)S(1)}, bf16[512,1280]{1,0:T(8,128)(2,1)S(1)}, u32[]{:S(2)}, u32[]{:S(2)}) collective-permute-start(bf16[512,1280]{1,0:T(8,128)(2,1)S(1)} %slice.54), channel_id=1, source_target_pairs={{0,4},{1,5},{2,6},{3,7},{4,0},{5,1},{6,2},{7,3},{8,12},{9,13},{10,... | collective-permute-start | bytes 3932168 | tf_op jit(solution)/shard_map/ppermute | solution.py:244
  184.4 85.0 %collective-permute-start.3 = (bf16[512,1280]{1,0:T(8,128)(2,1)S(1)}, bf16[512,1280]{1,0:T(8,128)(2,1)S(1)}, u32[]{:S(2)}, u32[]{:S(2)}) collective-permute-start(bf16[512,1280]{1,0:T(8,128)(2,1)S(1)} %slice.55), channel_id=1, source_target_pairs={{0,2},{1,3},{2,0},{3,1},{4,6},{5,7},{6,4},{7,5},{8,10},{9,11},{10,... | collective-permute-start | bytes 3932168 | tf_op jit(solution)/shard_map/ppermute | solution.py:244
  219.3 50.0 %copy-start.7 = (bf16[1024,1280]{1,0:T(8,128)(2,1)}, bf16[1024,1280]{1,0:T(8,128)(2,1)S(1)}, u32[]{:S(2)}) copy-start(bf16[1024,1280]{1,0:T(8,128)(2,1)S(1)} %collective-permute-done.9.refs_11_.refs_2_) | copy-start | bytes 7864324
  219.3 83.1 %collective-permute-start.32 = (bf16[1024,1280]{1,0:T(8,128)(2,1)}, bf16[1024,1280]{1,0:T(8,128)(2,1)}, u32[]{:S(2)}, u32[]{:S(2)}) collective-permute-start(bf16[1024,1280]{1,0:T(8,128)(2,1)} %collective-permute-done.30.refs_5_.refs_2_), channel_id=1, source_target_pairs={{0,1},{1,0},{2,3},{3,2},{4,5},{5,4},{6,7},{7,6},{8,9},{9,8},{10,11... | collective-permute-start | bytes 7864328 | tf_op jit(solution)/shard_map/ppermute | solution.py:244
  238.5 31.4 %copy-start.8 = (bf16[1024,1280]{1,0:T(8,128)(2,1)}, bf16[1024,1280]{1,0:T(8,128)(2,1)S(1)}, u32[]{:S(2)}) copy-start(bf16[1024,1280]{1,0:T(8,128)(2,1)S(1)} %collective-permute-done.10.refs_12_.refs_3_) | copy-start | bytes 7864324
  238.5 64.4 %collective-permute-start.5 = (bf16[1024,1280]{1,0:T(8,128)(2,1)}, bf16[1024,1280]{1,0:T(8,128)(2,1)}, u32[]{:S(2)}, u32[]{:S(2)}) collective-permute-start(bf16[1024,1280]{1,0:T(8,128)(2,1)} %collective-permute-done.refs_1_), channel_id=1, source_target_pairs={{0,1},{1,0},{2,3},{3,2},{4,5},{5,4},{6,7},{7,6},{8,9},{9,8},{10,11... | collective-permute-start | bytes 7864328 | tf_op jit(solution)/shard_map/ppermute | solution.py:244
  266.6 36.4 %collective-permute-start.6 = (bf16[1024,1280]{1,0:T(8,128)(2,1)}, bf16[1024,1280]{1,0:T(8,128)(2,1)}, u32[]{:S(2)}, u32[]{:S(2)}) collective-permute-start(bf16[1024,1280]{1,0:T(8,128)(2,1)} %collective-permute-done.1.refs_2_), channel_id=1, source_target_pairs={{0,1},{1,0},{2,3},{3,2},{4,5},{5,4},{6,7},{7,6},{8,9},{9,8},{10,11... | collective-permute-start | bytes 7864328 | tf_op jit(solution)/shard_map/ppermute | solution.py:244
  269.3 31.3 %collective-permute-start.11 = (bf16[512,1280]{1,0:T(8,128)(2,1)}, bf16[512,1280]{1,0:T(8,128)(2,1)}, u32[]{:S(2)}, u32[]{:S(2)}) collective-permute-start(bf16[512,1280]{1,0:T(8,128)(2,1)} %slice.56), channel_id=1, source_target_pairs={{0,4},{1,5},{2,6},{3,7},{4,0},{5,1},{6,2},{7,3},{8,12},{9,13},{10,... | collective-permute-start | bytes 3932168 | tf_op jit(solution)/shard_map/ppermute | solution.py:244
  271.4 31.0 %collective-permute-start.12 = (bf16[512,1280]{1,0:T(8,128)(2,1)}, bf16[512,1280]{1,0:T(8,128)(2,1)}, u32[]{:S(2)}, u32[]{:S(2)}) collective-permute-start(bf16[512,1280]{1,0:T(8,128)(2,1)} %slice.57), channel_id=1, source_target_pairs={{0,2},{1,3},{2,0},{3,1},{4,6},{5,7},{6,4},{7,5},{8,10},{9,11},{10,... | collective-permute-start | bytes 3932168 | tf_op jit(solution)/shard_map/ppermute | solution.py:244
  300.6 98.7 %collective-permute-start.13 = (bf16[1024,1280]{1,0:T(8,128)(2,1)}, bf16[1024,1280]{1,0:T(8,128)(2,1)}, u32[]{:S(2)}, u32[]{:S(2)}) collective-permute-start(bf16[1024,1280]{1,0:T(8,128)(2,1)} %add_convert_fusion.refs_10_.refs_1_), channel_id=1, source_target_pairs={{0,1},{1,0},{2,3},{3,2},{4,5},{5,4},{6,7},{7,6},{8,9},{9,8},{10,11... | collective-permute-start | bytes 7864328 | tf_op jit(solution)/shard_map/ppermute | solution.py:244
  302.4 98.4 %collective-permute-start.14 = (bf16[1024,1280]{1,0:T(8,128)(2,1)}, bf16[1024,1280]{1,0:T(8,128)(2,1)}, u32[]{:S(2)}, u32[]{:S(2)}) collective-permute-start(bf16[1024,1280]{1,0:T(8,128)(2,1)} %copy-done.7), channel_id=1, source_target_pairs={{0,1},{1,0},{2,3},{3,2},{4,5},{5,4},{6,7},{7,6},{8,9},{9,8},{10,11... | collective-permute-start | bytes 7864328 | tf_op jit(solution)/shard_map/ppermute | solution.py:244
  302.4 99.4 %collective-permute-start.15 = (bf16[1024,1280]{1,0:T(8,128)(2,1)}, bf16[1024,1280]{1,0:T(8,128)(2,1)}, u32[]{:S(2)}, u32[]{:S(2)}) collective-permute-start(bf16[1024,1280]{1,0:T(8,128)(2,1)} %copy-done.8), channel_id=1, source_target_pairs={{0,1},{1,0},{2,3},{3,2},{4,5},{5,4},{6,7},{7,6},{8,9},{9,8},{10,11... | collective-permute-start | bytes 7864328 | tf_op jit(solution)/shard_map/ppermute | solution.py:244
  302.9 62.7 %collective-permute-start.7 = (bf16[512,1280]{1,0:T(8,128)(2,1)}, bf16[512,1280]{1,0:T(8,128)(2,1)}, u32[]{:S(2)}, u32[]{:S(2)}) collective-permute-start(bf16[512,1280]{1,0:T(8,128)(2,1)} %copy-done.15), channel_id=1, source_target_pairs={{0,1},{1,0},{2,3},{3,2},{4,5},{5,4},{6,7},{7,6},{8,9},{9,8},{10,11... | collective-permute-start | bytes 3932168 | tf_op jit(solution)/shard_map/ppermute | solution.py:244
  303.0 62.8 %collective-permute-start.8 = (bf16[512,1280]{1,0:T(8,128)(2,1)}, bf16[512,1280]{1,0:T(8,128)(2,1)}, u32[]{:S(2)}, u32[]{:S(2)}) collective-permute-start(bf16[512,1280]{1,0:T(8,128)(2,1)} %copy-done.16), channel_id=1, source_target_pairs={{0,1},{1,0},{2,3},{3,2},{4,5},{5,4},{6,7},{7,6},{8,9},{9,8},{10,11... | collective-permute-start | bytes 3932168 | tf_op jit(solution)/shard_map/ppermute | solution.py:244
  365.7 36.1 %collective-permute-start.16 = (bf16[512,1280]{1,0:T(8,128)(2,1)}, bf16[512,1280]{1,0:T(8,128)(2,1)}, u32[]{:S(2)}, u32[]{:S(2)}) collective-permute-start(bf16[512,1280]{1,0:T(8,128)(2,1)} %collective-permute-done.11.refs_13_.refs_4_), channel_id=1, source_target_pairs={{0,1},{1,0},{2,3},{3,2},{4,5},{5,4},{6,7},{7,6},{8,9},{9,8},{10,11... | collective-permute-start | bytes 3932168 | tf_op jit(solution)/shard_map/ppermute | solution.py:244
  365.8 36.0 %collective-permute-start.17 = (bf16[512,1280]{1,0:T(8,128)(2,1)}, bf16[512,1280]{1,0:T(8,128)(2,1)}, u32[]{:S(2)}, u32[]{:S(2)}) collective-permute-start(bf16[512,1280]{1,0:T(8,128)(2,1)} %collective-permute-done.12.refs_14_.refs_5_), channel_id=1, source_target_pairs={{0,1},{1,0},{2,3},{3,2},{4,5},{5,4},{6,7},{7,6},{8,9},{9,8},{10,11... | collective-permute-start | bytes 3932168 | tf_op jit(solution)/shard_map/ppermute | solution.py:244
  399.3 207.6 %collective-permute-start.33 = (f32[2,2,2,2,40,640]{5,4,3,2,1,0:T(8,128)}, f32[2,2,2,2,40,640]{5,4,3,2,1,0:T(8,128)}, u32[]{:S(2)}, u32[]{:S(2)}) collective-permute-start(f32[2,2,2,2,40,640]{5,4,3,2,1,0:T(8,128)} %dynamic-slice_bitcast_fusion.1), channel_id=1, source_target_pairs={{0,4},{1,5},{2,6},{3,7},{4,0},{5,1},{6,2},{7,3},{8,12},{9,13},{10,... | collective-permute-start | bytes 4915208 | tf_op jit(solution)/shard_map/ppermute | solution.py:244
  400.8 210.0 %collective-permute-start.36 = (f32[2,2,2,2,40,640]{5,4,3,2,1,0:T(8,128)}, f32[2,2,2,2,40,640]{5,4,3,2,1,0:T(8,128)}, u32[]{:S(2)}, u32[]{:S(2)}) collective-permute-start(f32[2,2,2,2,40,640]{5,4,3,2,1,0:T(8,128)} %dynamic-slice_bitcast_fusion), channel_id=1, source_target_pairs={{0,2},{1,3},{2,0},{3,1},{4,6},{5,7},{6,4},{7,5},{8,10},{9,11},{10,... | collective-permute-start | bytes 4915208 | tf_op jit(solution)/shard_map/ppermute | solution.py:244
  474.9 65.1 %collective-permute-start.18 = (f32[320,640]{1,0:T(8,128)}, f32[320,640]{1,0:T(8,128)}, u32[]{:S(2)}, u32[]{:S(2)}) collective-permute-start(f32[320,640]{1,0:T(8,128)} %get-tuple-element.20), channel_id=1, source_target_pairs={{0,8},{1,9},{2,10},{3,11},{4,12},{5,13},{6,14},{7,15}} | collective-permute-start | bytes 2457608 | tf_op jit(solution)/shard_map/ppermute | solution.py:244
  506.7 35.2 %collective-permute-start.41 = (f32[160,1280]{1,0:T(8,128)}, f32[160,1280]{1,0:T(8,128)}, u32[]{:S(2)}, u32[]{:S(2)}) collective-permute-start(f32[160,1280]{1,0:T(8,128)} %get-tuple-element.16), channel_id=1, source_target_pairs={{0,8},{1,9},{2,10},{3,11},{4,12},{5,13},{6,14},{7,15}} | collective-permute-start | bytes 2457608 | tf_op jit(solution)/shard_map/ppermute | solution.py:244
  534.4 45.0 %collective-permute-start.53 = (f32[2,2,160,384]{3,2,1,0:T(8,128)S(1)}, f32[2,2,160,384]{3,2,1,0:T(8,128)S(1)}, u32[]{:S(2)}, u32[]{:S(2)}) collective-permute-start(f32[2,2,160,384]{3,2,1,0:T(8,128)S(1)} %dynamic-slice_bitcast_fusion.3), channel_id=1, source_target_pairs={{0,16},{1,17},{2,18},{3,19},{4,20},{5,21},{6,22},{7,23},{8,24},{9,... | collective-permute-start | bytes 2949128 | tf_op jit(solution)/shard_map/ppermute | solution.py:244
  537.7 41.7 %copy-start.6 = (f32[320,640]{1,0:T(8,128)S(1)}, f32[320,640]{1,0:T(8,128)}, u32[]{:S(2)}) copy-start(f32[320,640]{1,0:T(8,128)} %get-tuple-element.21) | copy-start | bytes 2457604
  539.9 40.3 %collective-permute-start.50 = (f32[2,2,160,384]{3,2,1,0:T(8,128)S(1)}, f32[2,2,160,384]{3,2,1,0:T(8,128)S(1)}, u32[]{:S(2)}, u32[]{:S(2)}) collective-permute-start(f32[2,2,160,384]{3,2,1,0:T(8,128)S(1)} %dynamic-slice_bitcast_fusion.4), channel_id=1, source_target_pairs={{0,4},{1,5},{2,6},{3,7},{4,0},{5,1},{6,2},{7,3},{8,12},{9,13},{10,... | collective-permute-start | bytes 2949128 | tf_op jit(solution)/shard_map/ppermute | solution.py:244
  541.9 39.5 %collective-permute-start.47 = (f32[2,2,160,512]{3,2,1,0:T(8,128)S(1)}, f32[2,2,160,512]{3,2,1,0:T(8,128)S(1)}, u32[]{:S(2)}, u32[]{:S(2)}) collective-permute-start(f32[2,2,160,512]{3,2,1,0:T(8,128)S(1)} %dynamic-slice_bitcast_fusion.2), channel_id=1, source_target_pairs={{0,2},{1,3},{2,0},{3,1},{4,6},{5,7},{6,4},{7,5},{8,10},{9,11},{10,... | collective-permute-start | bytes 3932168 | tf_op jit(solution)/shard_map/ppermute | solution.py:244
  579.4 33.7 %collective-permute-start.21 = (f32[320,640]{1,0:T(8,128)S(1)}, f32[320,640]{1,0:T(8,128)S(1)}, u32[]{:S(2)}, u32[]{:S(2)}) collective-permute-start(f32[320,640]{1,0:T(8,128)S(1)} %copy-done.6), channel_id=1, source_target_pairs={{24,16},{25,17},{26,18},{27,19},{28,20},{29,21},{30,22},{31,23}} | collective-permute-start | bytes 2457608 | tf_op jit(solution)/shard_map/ppermute | solution.py:244
  580.2 14.2 %collective-permute-start.54 = (f32[2,160,384]{2,1,0:T(8,128)S(1)}, f32[2,160,384]{2,1,0:T(8,128)S(1)}, u32[]{:S(2)}, u32[]{:S(2)}) collective-permute-start(f32[2,160,384]{2,1,0:T(8,128)S(1)} %dynamic-slice_bitcast_fusion.12), channel_id=1, source_target_pairs={{0,2},{1,3},{2,0},{3,1},{4,6},{5,7},{6,4},{7,5},{8,10},{9,11},{10,... | collective-permute-start | bytes 1474568 | tf_op jit(solution)/shard_map/ppermute | solution.py:244
  581.4 27.7 %copy-start.3 = (f32[2,2,2,2,2,40,640]{6,5,4,3,2,1,0:T(8,128)S(1)}, f32[2,2,2,2,2,40,640]{6,5,4,3,2,1,0:T(8,128)}, u32[]{:S(2)}) copy-start(f32[2,2,2,2,2,40,640]{6,5,4,3,2,1,0:T(8,128)} %copy-done.2) | copy-start | bytes 9830404
  581.5 21.8 %collective-permute-start.51 = (f32[2,160,384]{2,1,0:T(8,128)S(1)}, f32[2,160,384]{2,1,0:T(8,128)S(1)}, u32[]{:S(2)}, u32[]{:S(2)}) collective-permute-start(f32[2,160,384]{2,1,0:T(8,128)S(1)} %dynamic-slice_bitcast_fusion.13), channel_id=1, source_target_pairs={{0,2},{1,3},{2,0},{3,1},{4,6},{5,7},{6,4},{7,5},{8,10},{9,11},{10,... | collective-permute-start | bytes 1474568 | tf_op jit(solution)/shard_map/ppermute | solution.py:244
  594.4 32.4 %collective-permute-start.44 = (f32[160,1280]{1,0:T(8,128)S(1)}, f32[160,1280]{1,0:T(8,128)S(1)}, u32[]{:S(2)}, u32[]{:S(2)}) collective-permute-start(f32[160,1280]{1,0:T(8,128)S(1)} %get-tuple-element.17), channel_id=1, source_target_pairs={{24,16},{25,17},{26,18},{27,19},{28,20},{29,21},{30,22},{31,23}} | collective-permute-start | bytes 2457608 | tf_op jit(solution)/shard_map/ppermute | solution.py:244
  603.2 23.3 %collective-permute-start.19 = (f32[320,640]{1,0:T(8,128)S(1)}, f32[320,640]{1,0:T(8,128)S(1)}, u32[]{:S(2)}, u32[]{:S(2)}) collective-permute-start(f32[320,640]{1,0:T(8,128)S(1)} %bitcast_add_fusion.14), channel_id=1, source_target_pairs={{0,8},{1,9},{2,10},{3,11},{4,12},{5,13},{6,14},{7,15},{8,16},{9,17... | collective-permute-start | bytes 2457608 | tf_op jit(solution)/shard_map/ppermute | solution.py:244
  606.9 44.8 %collective-permute-start.42 = (f32[160,1280]{1,0:T(8,128)S(1)}, f32[160,1280]{1,0:T(8,128)S(1)}, u32[]{:S(2)}, u32[]{:S(2)}) collective-permute-start(f32[160,1280]{1,0:T(8,128)S(1)} %bitcast_add_fusion.7), channel_id=1, source_target_pairs={{0,8},{1,9},{2,10},{3,11},{4,12},{5,13},{6,14},{7,15},{8,16},{9,17... | collective-permute-start | bytes 2457608 | tf_op jit(solution)/shard_map/ppermute | solution.py:244
  610.8 41.6 %collective-permute-start.48 = (f32[2,160,512]{2,1,0:T(8,128)S(1)}, f32[2,160,512]{2,1,0:T(8,128)S(1)}, u32[]{:S(2)}, u32[]{:S(2)}) collective-permute-start(f32[2,160,512]{2,1,0:T(8,128)S(1)} %dynamic-slice_bitcast_fusion.11), channel_id=1, source_target_pairs={{0,4},{1,5},{2,6},{3,7},{4,0},{5,1},{6,2},{7,3},{8,12},{9,13},{10,... | collective-permute-start | bytes 1966088 | tf_op jit(solution)/shard_map/ppermute | solution.py:244
  613.1 40.7 %collective-permute-start.55 = (f32[160,384]{1,0:T(8,128)S(1)}, f32[160,384]{1,0:T(8,128)S(1)}, u32[]{:S(2)}, u32[]{:S(2)}) collective-permute-start(f32[160,384]{1,0:T(8,128)S(1)} %dynamic-slice_bitcast_fusion.18), channel_id=1, source_target_pairs={{0,4},{1,5},{2,6},{3,7},{4,0},{5,1},{6,2},{7,3},{8,12},{9,13},{10,... | collective-permute-start | bytes 737288 | tf_op jit(solution)/shard_map/ppermute | solution.py:244
  626.5 32.1 %collective-permute-start.52 = (f32[160,384]{1,0:T(8,128)S(1)}, f32[160,384]{1,0:T(8,128)S(1)}, u32[]{:S(2)}, u32[]{:S(2)}) collective-permute-start(f32[160,384]{1,0:T(8,128)S(1)} %dynamic-slice_bitcast_fusion.19), channel_id=1, source_target_pairs={{0,16},{1,17},{2,18},{3,19},{4,20},{5,21},{6,22},{7,23},{8,24},{9,... | collective-permute-start | bytes 737288 | tf_op jit(solution)/shard_map/ppermute | solution.py:244
  626.8 50.2 %collective-permute-start.34 = (f32[2,2,2,40,640]{4,3,2,1,0:T(8,128)S(1)}, f32[2,2,2,40,640]{4,3,2,1,0:T(8,128)S(1)}, u32[]{:S(2)}, u32[]{:S(2)}) collective-permute-start(f32[2,2,2,40,640]{4,3,2,1,0:T(8,128)S(1)} %dynamic-slice_bitcast_fusion.8), channel_id=1, source_target_pairs={{0,2},{1,3},{2,0},{3,1},{4,6},{5,7},{6,4},{7,5},{8,10},{9,11},{10,... | collective-permute-start | bytes 2457608 | tf_op jit(solution)/shard_map/ppermute | solution.py:244
  651.7 45.2 %collective-permute-start.37 = (f32[2,2,2,40,640]{4,3,2,1,0:T(8,128)S(1)}, f32[2,2,2,40,640]{4,3,2,1,0:T(8,128)S(1)}, u32[]{:S(2)}, u32[]{:S(2)}) collective-permute-start(f32[2,2,2,40,640]{4,3,2,1,0:T(8,128)S(1)} %dynamic-slice_bitcast_fusion.7), channel_id=1, source_target_pairs={{0,4},{1,5},{2,6},{3,7},{4,0},{5,1},{6,2},{7,3},{8,12},{9,13},{10,... | collective-permute-start | bytes 2457608 | tf_op jit(solution)/shard_map/ppermute | solution.py:244
  652.4 45.6 %collective-permute-start.22 = (f32[320,640]{1,0:T(8,128)S(1)}, f32[320,640]{1,0:T(8,128)S(1)}, u32[]{:S(2)}, u32[]{:S(2)}) collective-permute-start(f32[320,640]{1,0:T(8,128)S(1)} %get-tuple-element.19), channel_id=1, source_target_pairs={{16,8},{17,9},{18,10},{19,11},{20,12},{21,13},{22,14},{23,15},{24,... | collective-permute-start | bytes 2457608 | tf_op jit(solution)/shard_map/ppermute | solution.py:244
  653.8 21.7 %collective-permute-start.49 = (f32[160,512]{1,0:T(8,128)S(1)}, f32[160,512]{1,0:T(8,128)S(1)}, u32[]{:S(2)}, u32[]{:S(2)}) collective-permute-start(f32[160,512]{1,0:T(8,128)S(1)} %dynamic-slice_bitcast_fusion.17), channel_id=1, source_target_pairs={{0,16},{1,17},{2,18},{3,19},{4,20},{5,21},{6,22},{7,23},{8,24},{9,... | collective-permute-start | bytes 983048 | tf_op jit(solution)/shard_map/ppermute | solution.py:244
  658.7 81.5 %collective-permute-start.20 = (f32[320,640]{1,0:T(8,128)S(1)}, f32[320,640]{1,0:T(8,128)S(1)}, u32[]{:S(2)}, u32[]{:S(2)}) collective-permute-start(f32[320,640]{1,0:T(8,128)S(1)} %get-tuple-element.18), channel_id=1, source_target_pairs={{0,8},{1,9},{2,10},{3,11},{4,12},{5,13},{6,14},{7,15},{8,16},{9,17... | collective-permute-start | bytes 2457608 | tf_op jit(solution)/shard_map/ppermute | solution.py:244
  675.6 61.0 %collective-permute-start.45 = (f32[160,1280]{1,0:T(8,128)S(1)}, f32[160,1280]{1,0:T(8,128)S(1)}, u32[]{:S(2)}, u32[]{:S(2)}) collective-permute-start(f32[160,1280]{1,0:T(8,128)S(1)} %get-tuple-element.15), channel_id=1, source_target_pairs={{16,8},{17,9},{18,10},{19,11},{20,12},{21,13},{22,14},{23,15},{24,... | collective-permute-start | bytes 2457608 | tf_op jit(solution)/shard_map/ppermute | solution.py:244
  677.0 86.9 %collective-permute-start.43 = (f32[160,1280]{1,0:T(8,128)S(1)}, f32[160,1280]{1,0:T(8,128)S(1)}, u32[]{:S(2)}, u32[]{:S(2)}) collective-permute-start(f32[160,1280]{1,0:T(8,128)S(1)} %get-tuple-element.14), channel_id=1, source_target_pairs={{0,8},{1,9},{2,10},{3,11},{4,12},{5,13},{6,14},{7,15},{8,16},{9,17... | collective-permute-start | bytes 2457608 | tf_op jit(solution)/shard_map/ppermute | solution.py:244
  696.9 34.6 %collective-permute-start.35 = (f32[2,2,40,640]{3,2,1,0:T(8,128)S(1)}, f32[2,2,40,640]{3,2,1,0:T(8,128)S(1)}, u32[]{:S(2)}, u32[]{:S(2)}) collective-permute-start(f32[2,2,40,640]{3,2,1,0:T(8,128)S(1)} %dynamic-slice_bitcast_fusion.15), channel_id=1, source_target_pairs={{0,16},{1,17},{2,18},{3,19},{4,20},{5,21},{6,22},{7,23},{8,24},{9,... | collective-permute-start | bytes 1228808 | tf_op jit(solution)/shard_map/ppermute | solution.py:244
  698.0 37.9 %collective-permute-start.38 = (f32[2,2,40,640]{3,2,1,0:T(8,128)S(1)}, f32[2,2,40,640]{3,2,1,0:T(8,128)S(1)}, u32[]{:S(2)}, u32[]{:S(2)}) collective-permute-start(f32[2,2,40,640]{3,2,1,0:T(8,128)S(1)} %dynamic-slice_bitcast_fusion.14), channel_id=1, source_target_pairs={{0,16},{1,17},{2,18},{3,19},{4,20},{5,21},{6,22},{7,23},{8,24},{9,... | collective-permute-start | bytes 1228808 | tf_op jit(solution)/shard_map/ppermute | solution.py:244
  731.5 23.0 %collective-permute-start.23 = (f32[320,640]{1,0:T(8,128)S(1)}, f32[320,640]{1,0:T(8,128)S(1)}, u32[]{:S(2)}, u32[]{:S(2)}) collective-permute-start(f32[320,640]{1,0:T(8,128)S(1)} %bitcast_add_fusion.13), channel_id=1, source_target_pairs={{8,0},{9,1},{10,2},{11,3},{12,4},{13,5},{14,6},{15,7},{16,8},{17,9... | collective-permute-start | bytes 2457608 | tf_op jit(solution)/shard_map/ppermute | solution.py:244
  736.0 24.8 %collective-permute-start.39 = (f32[2,40,1280]{2,1,0:T(8,128)S(1)}, f32[2,40,1280]{2,1,0:T(8,128)S(1)}, u32[]{:S(2)}, u32[]{:S(2)}) collective-permute-start(f32[2,40,1280]{2,1,0:T(8,128)S(1)} %fusion.82), channel_id=1, source_target_pairs={{0,8},{1,9},{2,10},{3,11},{4,12},{5,13},{6,14},{7,15},{8,0},{9,1},... | collective-permute-start | bytes 1228808 | tf_op jit(solution)/shard_map/ppermute | solution.py:244
  736.6 36.7 %collective-permute-start.46 = (f32[160,1280]{1,0:T(8,128)S(1)}, f32[160,1280]{1,0:T(8,128)S(1)}, u32[]{:S(2)}, u32[]{:S(2)}) collective-permute-start(f32[160,1280]{1,0:T(8,128)S(1)} %bitcast_add_fusion.6), channel_id=1, source_target_pairs={{8,0},{9,1},{10,2},{11,3},{12,4},{13,5},{14,6},{15,7},{16,8},{17,9... | collective-permute-start | bytes 2457608 | tf_op jit(solution)/shard_map/ppermute | solution.py:244
  754.7 8.0 %collective-permute-start.24 = (f32[2,2,40,640]{3,2,1,0:T(8,128)S(1)}, f32[2,2,40,640]{3,2,1,0:T(8,128)S(1)}, u32[]{:S(2)}, u32[]{:S(2)}) collective-permute-start(f32[2,2,40,640]{3,2,1,0:T(8,128)S(1)} %dynamic-slice_bitcast_fusion.16), channel_id=1, source_target_pairs={{0,4},{1,5},{2,6},{3,7},{4,0},{5,1},{6,2},{7,3},{8,12},{9,13},{10,... | collective-permute-start | bytes 1228808 | tf_op jit(solution)/shard_map/ppermute | solution.py:244
  760.9 14.6 %collective-permute-start.40 = (f32[2,40,1280]{2,1,0:T(8,128)S(1)}, f32[2,40,1280]{2,1,0:T(8,128)S(1)}, u32[]{:S(2)}, u32[]{:S(2)}) collective-permute-start(f32[2,40,1280]{2,1,0:T(8,128)S(1)} %fusion.78), channel_id=1, source_target_pairs={{0,1},{1,0},{2,3},{3,2},{4,5},{5,4},{6,7},{7,6},{8,9},{9,8},{10,11... | collective-permute-start | bytes 1228808 | tf_op jit(solution)/shard_map/ppermute | solution.py:244
  762.8 11.9 %collective-permute-start.25 = (f32[2,2,40,640]{3,2,0,1:T(8,128)S(1)}, f32[2,2,40,640]{3,2,0,1:T(8,128)S(1)}, u32[]{:S(2)}, u32[]{:S(2)}) collective-permute-start(f32[2,2,40,640]{3,2,0,1:T(8,128)S(1)} %fusion.90), channel_id=1, source_target_pairs={{0,2},{1,3},{2,0},{3,1},{4,6},{5,7},{6,4},{7,5},{8,10},{9,11},{10,... | collective-permute-start | bytes 1228808 | tf_op jit(solution)/shard_map/ppermute | solution.py:244
  775.6 5.5 collective-permute-start.26
  (9 other events, 64.6 us)

commit v2 on v1

--- a/solution.py
+++ b/solution.py
@@ -278,16 +278,19 @@
         def line_reduce(arr):
             right = [[(i, i + 8) for i in range(n) if i // 8 <= min(s, 2)] for s in range(3)]
             left = [[(i, i - 8) for i in range(n) if 3 - i // 8 <= min(s, 2)] for s in range(3)]
+
+            def chunk(k):
+                return lax.dynamic_index_in_dim(arr, jnp.clip(k, 0, 3), 0, keepdims=False)
+
+            mine = lax.optimization_barrier([chunk(3 - s + z) for s in range(3)] + [chunk(s + z - 3) for s in range(3)] + [chunk(z)])
             recv_r = recv_l = None
             for s in range(3):
-                send_r = lax.dynamic_index_in_dim(arr, jnp.clip(3 - s + z, 0, 3), 0, keepdims=False)
-                send_l = lax.dynamic_index_in_dim(arr, jnp.clip(s + z - 3, 0, 3), 0, keepdims=False)
+                send_r, send_l = mine[s], mine[3 + s]
                 if s:
                     send_r, send_l = send_r + recv_r, send_l + recv_l
                 recv_r = permute(send_r, right[s])
                 recv_l = permute(send_l, left[s])
-            own = lax.dynamic_index_in_dim(arr, z, 0, keepdims=False)
-            return own + recv_r + recv_l
+            return mine[6] + recv_r + recv_l
 
         def spread(arr, axis, b):
             keep = lax.dynamic_index_in_dim(arr, bit(b), axis, keepdims=False)

time: 799 us -> 690 us (0.86)
  waiting for transfers between devices: 285 us -> 146 us
  local copies, waits for them, and re-layouts: 32.6 us -> 50.2 us
  starting transfers between devices: 76 us -> 88.7 us
  other arithmetic: 13.3 us -> 21.5 us
    ppermute x56, waiting for transfers between devices: 285 us -> 146 us  [permute(): return lax.ppermute(v, 'data', pairs)]
    ppermute x56, starting transfers between devices: 76 us -> 88.7 us  [permute(): return lax.ppermute(v, 'data', pairs)]
  transfers between devices with their start and end apart: 56 -> 56, of which waited for: 19 -> 11; matrix products, arithmetic and copies ran while one was open for 17% -> 23% of each run, Pallas kernels for 30% -> 24%
where the time goes in v2:
time: 690 us; the launch traced here: 679 us
  Pallas kernels  236 us (34%)
  waiting for transfers between devices  146 us (21%)
  matrix products  134 us (19%)
  starting transfers between devices  88.7 us (13%)
  local copies, waits for them, and re-layouts  50.2 us (7%)
  other arithmetic  21.5 us (3%)
    pallas_call x6, Pallas kernels, call(): pl.pallas_call(kernel, out_shape=out_shape, in_specs=in_specs, out_specs=...  236 us
    ppermute x56, waiting for transfers between devices, permute(): return lax.ppermute(v, 'data', pairs)  146 us
    dot_general x6, matrix products, dot(): return lax.dot_general(a, b, (dims, ((), ())), preferred_element_type=F32)  134 us
    ppermute x56, starting transfers between devices, permute(): return lax.ppermute(v, 'data', pairs)  88.7 us
    slice x3, local copies, waits for them, and re-layouts, scatter(): lax.slice_in_dim(arr, at, at + size, axis=arr.ndim - 1)  13.9 us
  transfers between devices with their start and end apart: 56, of which 11 were waited for; matrix products, arithmetic and copies ran while one was open for 23% of the time, Pallas kernels for 24%

profile of v2, /device:TPU:14, one launch (start us, length us, event | category | flops | bytes accessed | tf_op | source)
XLA Modules:
  0.0 678.7 jit_solution(1870363983274573667)
XLA Ops:
  0.6 20.1 %fusion.141 = bf16[1024,5120]{1,0:T(8,128)(2,1)S(1)} fusion(bf16[1024,1280]{1,0:T(8,128)(2,1)} %refs_0_.3, bf16[2,1280,5120]{2,1,0:T(8,128)(2,1)} %refs_4_.1), kind=kOutput, calls=%fused_computation.20.clone.clone.clone.clone.2 | convolution fusion | flops 13479444480 | bytes 26214400 | tf_op jit(solution)/shard_map/dot_general | solution.py:22
  20.8 17.1 %add_convert_fusion.2.refs_0_ = bf16[1024,1280]{1,0:T(8,128)(2,1)} fusion(bf16[1024,1280]{1,0:T(8,128)(2,1)} %refs_0_.3, bf16[2,5120,1280]{2,1,0:T(8,128)(2,1)} %refs_9_.1, bf16[1024,5120]{1,0:T(8,128)(2,1)S(1)} %fusion.141), kind=kOutput, calls=%fused_computation.56 | convolution fusion | flops 13425704960 | bytes 28835840 | tf_op jit(solution)/shard_map/dot_general | solution.py:22
  39.0 19.8 %fusion.49 = bf16[1024,5120]{1,0:T(8,128)(2,1)} fusion(bf16[1024,1280]{1,0:T(8,128)(2,1)} %add_convert_fusion.2.refs_0_, bf16[2,1280,5120]{2,1,0:T(8,128)(2,1)} %refs_4_.1), kind=kOutput, calls=%fused_computation.52 | convolution fusion | flops 13427015680 | bytes 26214400 | tf_op jit(solution)/shard_map/dot_general | solution.py:22
  58.9 26.4 %multiply_convert_fusion.refs_4_.refs_1_ = bf16[1024,1280]{1,0:T(8,128)(2,1)} fusion(bf16[1024,1280]{1,0:T(8,128)(2,1)S(1)} %copy-done.24, bf16[2,5120,1280]{2,1,0:T(8,128)(2,1)} %refs_9_.1, bf16[1024,5120]{1,0:T(8,128)(2,1)} %fusion.49, bf16[1024,1280]{1,0:T(8,128)(2,1)} %add_convert_fusion.2.refs_0_), kind=kOutput, calls=%fused_computation.54 | convolution fusion | flops 13484687360 | bytes 31457280 | tf_op jit(solution)/shard_map/dot_general | solution.py:22
  85.3 1.9 collective-permute-start.30
  87.2 29.8 %fusion.137 = bf16[1024,5120]{1,0:T(8,128)(2,1)} fusion(bf16[1024,5120]{1,0:T(8,128)(2,1)} %fusion.49, bf16[1024,1280]{1,0:T(8,128)(2,1)} %multiply_convert_fusion.refs_4_.refs_1_, bf16[2,5120,1280]{2,1,0:T(8,128)(2,1)} %refs_9_.1), kind=kOutput, calls=%fused_computation.13.clone.clone.clone.clone.2 | convolution fusion | flops 13542359040 | bytes 36700160 | tf_op jit(solution)/shard_map/dot_general | solution.py:22
  116.9 21.1 %add_convert_fusion.refs_10_.refs_1_ = bf16[1024,1280]{1,0:T(8,128)(2,1)} fusion(bf16[1024,1280]{1,0:T(8,128)(2,1)} %multiply_convert_fusion.refs_4_.refs_1_, bf16[2,1280,5120]{2,1,0:T(8,128)(2,1)} %refs_4_.1, bf16[1024,5120]{1,0:T(8,128)(2,1)} %fusion.137), kind=kOutput, calls=%fused_computation.53 | convolution fusion | flops 13425704960 | bytes 28835840 | tf_op jit(solution)/shard_map/dot_general | solution.py:22
  138.0 1.6 collective-permute-start.9
  139.6 1.5 collective-permute-start.10
  141.1 11.8 %collective-permute-done.30.refs_5_.refs_2_ = bf16[1024,1280]{1,0:T(8,128)(2,1)} collective-permute-done((bf16[1024,1280]{1,0:T(8,128)(2,1)}, bf16[1024,1280]{1,0:T(8,128)(2,1)}, u32[]{:S(2)}, u32[]{:S(2)}) %collective-permute-start.30) | collective-permute-done | bytes 2621472 | tf_op jit(solution)/shard_map/ppermute | solution.py:244
  153.5 43.4 %collective-permute-done.9.refs_11_.refs_2_ = bf16[1024,1280]{1,0:T(8,128)(2,1)} collective-permute-done((bf16[1024,1280]{1,0:T(8,128)(2,1)}, bf16[1024,1280]{1,0:T(8,128)(2,1)}, u32[]{:S(2)}, u32[]{:S(2)}) %collective-permute-start.9) | collective-permute-done | bytes 2621472 | tf_op jit(solution)/shard_map/ppermute | solution.py:244
  196.9 2.5 slice.54
  199.4 1.5 collective-permute-start.2
  200.9 2.5 slice.55
  203.4 2.5 slice.56
  205.8 2.5 slice.57
  208.3 1.5 collective-permute-start.3
  209.8 27.1 %shard_map.61 = (bf16[4096,1280]{1,0:T(8,128)(2,1)}, bf16[4096,1280]{1,0:T(8,128)(2,1)}) custom-call(bf16[1024,1280]{1,0:T(8,128)(2,1)} %add_convert_fusion.2.refs_0_, bf16[1024,1280]{1,0:T(8,128)(2,1)} %collective-permute-done.27.refs_1_, bf16[1024,1280]{1,0:T(8,128)(2,1)} %collective-permute-done.28.refs_2_, ...), custom_call_target="tpu_custom_call" | custom-call | flops 13421772800 | bytes 36700160 | tf_op jit(solution)/shard_map/pallas_call | solution.py:52
  238.5 55.2 %shard_map.62 = f32[1280,1280]{1,0:T(8,128)} custom-call(bf16[1024,1280]{1,0:T(8,128)(2,1)} %add_convert_fusion.2.refs_0_, bf16[1024,1280]{1,0:T(8,128)(2,1)} %collective-permute-done.27.refs_1_, bf16[1024,1280]{1,0:T(8,128)(2,1)} %collective-permute-done.28.refs_2_, bf16[1024,1280]{1,0:T(8,128)(2,1)} %collective-permute-done.29.refs_3_, ...), custom_call_target="tpu_custom_call" | custom-call | flops 26843545600 | bytes 57671680 | tf_op jit(solution)/shard_map/pallas_call | solution.py:52
  294.3 6.1 fusion.107
  301.0 23.8 %shard_map.64 = f32[1280,1280]{1,0:T(8,128)} custom-call(bf16[4096,1280]{1,0:T(8,128)(2,1)} %get-tuple-element.37.refs_0_, bf16[1024,1280]{1,0:T(8,128)(2,1)} %multiply_convert_fusion.refs_4_.refs_1_, bf16[1024,1280]{1,0:T(8,128)(2,1)} %collective-permute-done.30.refs_5_.refs_2_, bf16[1024,1280]{1,0:T(8,128)(2,1)} %collective-permute-done.31.refs_6_.refs_3_, ...), custom_call_target="tpu_custom_call" | custom-call | flops 13421772800 | bytes 20971520 | tf_op jit(solution)/shard_map/pallas_call | solution.py:52
  325.5 4.4 fusion.106
  329.8 3.5 slice.60
  333.3 31.8 %shard_map.59 = (bf16[8192,640]{1,0:T(8,128)(2,1)}, bf16[8192,640]{1,0:T(8,128)(2,1)}) custom-call(bf16[1024,1280]{1,0:T(8,128)(2,1)} %refs_0_.3, bf16[1024,1280]{1,0:T(8,128)(2,1)} %collective-permute-done.refs_1_, bf16[1024,1280]{1,0:T(8,128)(2,1)} %collective-permute-done.1.refs_2_, bf16[512,1280]{1,0:T(8,128)(2,1)} %collective-permute-done.2.refs_3_, ...), custom_call_target="tpu_custom_call" | custom-call | flops 13421772800 | bytes 47185920 | tf_op jit(solution)/shard_map/pallas_call | solution.py:52
  365.1 70.3 %shard_map.60 = f32[1280,640]{1,0:T(8,128)} custom-call(bf16[1024,1280]{1,0:T(8,128)(2,1)} %refs_0_.3, bf16[1024,1280]{1,0:T(8,128)(2,1)} %collective-permute-done.refs_1_, bf16[1024,1280]{1,0:T(8,128)(2,1)} %collective-permute-done.1.refs_2_, bf16[512,1280]{1,0:T(8,128)(2,1)} %collective-permute-done.2.refs_3_, ...), custom_call_target="tpu_custom_call" | custom-call | flops 26843545600 | bytes 78643200 | tf_op jit(solution)/shard_map/pallas_call | solution.py:52
  435.5 5.3 dynamic-slice_bitcast_fusion.14
  440.9 1.7 collective-permute-start.21
  444.8 4.6 collective-permute-start.53
  450.5 1.5 collective-permute-start.50
  453.2 1.5 collective-permute-start.47
  454.7 28.1 %shard_map.63 = f32[640,1280]{1,0:T(8,128)} custom-call(bf16[8192,640]{1,0:T(8,128)(2,1)} %get-tuple-element.29.refs_0_, bf16[1024,1280]{1,0:T(8,128)(2,1)} %add_convert_fusion.refs_10_.refs_1_, bf16[1024,1280]{1,0:T(8,128)(2,1)} %collective-permute-done.9.refs_11_.refs_2_, bf16[1024,1280]{1,0:T(8,128)(2,1)} %collective-permute-done.10.refs_12_.refs_3_, ...), custom_call_target="tpu_custom_call" | custom-call | flops 13421772800 | bytes 31457280 | tf_op jit(solution)/shard_map/pallas_call | solution.py:52
  482.8 4.8 dynamic-slice_bitcast_fusion.5
  489.7 2.4 collective-permute-done.53
  493.4 1.3 bitcast_add_fusion.3
  494.8 1.6 collective-permute-start.33
  499.7 1.5 collective-permute-start.54
  503.0 10.4 %collective-permute-done.41 = f32[160,1280]{1,0:T(8,128)S(1)} collective-permute-done((f32[160,1280]{1,0:T(8,128)S(1)}, f32[160,1280]{1,0:T(8,128)S(1)}, u32[]{:S(2)}, u32[]{:S(2)}) %collective-permute-start.41) | collective-permute-done | bytes 819232 | tf_op jit(solution)/shard_map/ppermute | solution.py:244
  514.3 1.5 collective-permute-start.36
  515.9 1.6 add.306
  517.5 1.8 add.303
  520.9 1.6 collective-permute-start.22
  522.5 1.6 bitcast_add_fusion.2
  524.2 4.7 collective-permute-start.19
  532.5 4.9 collective-permute-start.42
  537.5 6.7 collective-permute-done.22
  544.2 1.5 collective-permute-start.48
  545.7 1.7 bitcast_add_fusion.1
  547.5 1.5 collective-permute-start.55
  549.1 14.8 %collective-permute-done.45 = f32[160,1280]{1,0:T(8,128)S(1)} collective-permute-done((f32[160,1280]{1,0:T(8,128)S(1)}, f32[160,1280]{1,0:T(8,128)S(1)}, u32[]{:S(2)}, u32[]{:S(2)}) %collective-permute-start.45) | collective-permute-done | bytes 819232 | tf_op jit(solution)/shard_map/ppermute | solution.py:244
  564.6 1.7 bitcast_add_fusion
  566.3 7.5 %collective-permute-done.42 = f32[160,1280]{1,0:T(8,128)S(1)} collective-permute-done((f32[160,1280]{1,0:T(8,128)S(1)}, f32[160,1280]{1,0:T(8,128)S(1)}, u32[]{:S(2)}, u32[]{:S(2)}) %collective-permute-start.42) | collective-permute-done | bytes 819232 | tf_op jit(solution)/shard_map/ppermute | solution.py:244
  573.8 1.5 collective-permute-start.37
  575.4 1.9 collective-permute-start.23
  577.5 4.0 collective-permute-start.49
  581.6 1.9 collective-permute-start.20
  583.6 13.5 %collective-permute-done.49 = f32[160,512]{1,0:T(8,128)S(1)} collective-permute-done((f32[160,512]{1,0:T(8,128)S(1)}, f32[160,512]{1,0:T(8,128)S(1)}, u32[]{:S(2)}, u32[]{:S(2)}) %collective-permute-start.49) | collective-permute-done | bytes 327712 | tf_op jit(solution)/shard_map/ppermute | solution.py:244
  597.0 23.6 %collective-permute-start.46 = (f32[160,1280]{1,0:T(8,128)S(1)}, f32[160,1280]{1,0:T(8,128)S(1)}, u32[]{:S(2)}, u32[]{:S(2)}) collective-permute-start(f32[160,1280]{1,0:T(8,128)S(1)} %add.331), channel_id=1, source_target_pairs={{8,0},{9,1},{10,2},{11,3},{12,4},{13,5},{14,6},{15,7},{16,8},{17,9... | collective-permute-start | bytes 2457608 | tf_op jit(solution)/shard_map/ppermute | solution.py:244
  620.8 1.9 collective-permute-start.43
  623.1 3.0 collective-permute-start.38
  626.3 2.5 collective-permute-start.24
  628.8 23.7 %collective-permute-done.35 = f32[2,2,40,640]{3,2,1,0:T(8,128)S(1)} collective-permute-done((f32[2,2,40,640]{3,2,1,0:T(8,128)S(1)}, f32[2,2,40,640]{3,2,1,0:T(8,128)S(1)}, u32[]{:S(2)}, u32[]{:S(2)}) %collective-permute-start.35) | collective-permute-done | bytes 409632 | tf_op jit(solution)/shard_map/ppermute | solution.py:244
  652.5 4.3 collective-permute-done.38
  658.0 7.0 %collective-permute-done.39 = f32[2,40,1280]{2,1,0:T(8,128)S(1)} collective-permute-done((f32[2,40,1280]{2,1,0:T(8,128)S(1)}, f32[2,40,1280]{2,1,0:T(8,128)S(1)}, u32[]{:S(2)}, u32[]{:S(2)}) %collective-permute-start.39) | collective-permute-done | bytes 409632 | tf_op jit(solution)/shard_map/ppermute | solution.py:244
  671.5 1.8 stack_reshape.7
  (181 shorter events, 38.7 us)
Async XLA Ops:
  37.8 21.0 %copy-start.24 = (bf16[1024,1280]{1,0:T(8,128)(2,1)S(1)}, bf16[1024,1280]{1,0:T(8,128)(2,1)}, u32[]{:S(2)}) copy-start(bf16[1024,1280]{1,0:T(8,128)(2,1)} %param.5) | copy-start | bytes 7864324
  37.9 100.2 %collective-permute-start.27 = (bf16[1024,1280]{1,0:T(8,128)(2,1)}, bf16[1024,1280]{1,0:T(8,128)(2,1)}, u32[]{:S(2)}, u32[]{:S(2)}) collective-permute-start(bf16[1024,1280]{1,0:T(8,128)(2,1)} %add_convert_fusion.2.refs_0_), channel_id=1, source_target_pairs={{0,8},{1,9},{2,10},{3,11},{4,12},{5,13},{6,14},{7,15},{8,0},{9,1},... | collective-permute-start | bytes 7864328 | tf_op jit(solution)/shard_map/ppermute | solution.py:244
  38.3 101.3 %collective-permute-start.28 = (bf16[1024,1280]{1,0:T(8,128)(2,1)}, bf16[1024,1280]{1,0:T(8,128)(2,1)}, u32[]{:S(2)}, u32[]{:S(2)}) collective-permute-start(bf16[1024,1280]{1,0:T(8,128)(2,1)} %add_convert_fusion.2.refs_0_), channel_id=1, source_target_pairs={{0,1},{1,0},{2,3},{3,2},{4,5},{5,4},{6,7},{7,6},{8,9},{9,8},{10,11... | collective-permute-start | bytes 7864328 | tf_op jit(solution)/shard_map/ppermute | solution.py:244
  38.3 114.7 %collective-permute-start = (bf16[1024,1280]{1,0:T(8,128)(2,1)}, bf16[1024,1280]{1,0:T(8,128)(2,1)}, u32[]{:S(2)}, u32[]{:S(2)}) collective-permute-start(bf16[1024,1280]{1,0:T(8,128)(2,1)} %refs_0_.3), channel_id=1, source_target_pairs={{0,2},{1,3},{2,0},{3,1},{4,6},{5,7},{6,4},{7,5},{8,10},{9,11},{10,... | collective-permute-start | bytes 7864328 | tf_op jit(solution)/shard_map/ppermute | solution.py:244
  38.8 114.6 %collective-permute-start.1 = (bf16[1024,1280]{1,0:T(8,128)(2,1)}, bf16[1024,1280]{1,0:T(8,128)(2,1)}, u32[]{:S(2)}, u32[]{:S(2)}) collective-permute-start(bf16[1024,1280]{1,0:T(8,128)(2,1)} %refs_0_.3), channel_id=1, source_target_pairs={{0,4},{1,5},{2,6},{3,7},{4,0},{5,1},{6,2},{7,3},{8,12},{9,13},{10,... | collective-permute-start | bytes 7864328 | tf_op jit(solution)/shard_map/ppermute | solution.py:244
  85.3 67.7 %collective-permute-start.30 = (bf16[1024,1280]{1,0:T(8,128)(2,1)}, bf16[1024,1280]{1,0:T(8,128)(2,1)}, u32[]{:S(2)}, u32[]{:S(2)}) collective-permute-start(bf16[1024,1280]{1,0:T(8,128)(2,1)} %multiply_convert_fusion.refs_4_.refs_1_), channel_id=1, source_target_pairs={{0,8},{1,9},{2,10},{3,11},{4,12},{5,13},{6,14},{7,15},{8,0},{9,1},... | collective-permute-start | bytes 7864328 | tf_op jit(solution)/shard_map/ppermute | solution.py:244
  138.0 58.9 %collective-permute-start.9 = (bf16[1024,1280]{1,0:T(8,128)(2,1)}, bf16[1024,1280]{1,0:T(8,128)(2,1)}, u32[]{:S(2)}, u32[]{:S(2)}) collective-permute-start(bf16[1024,1280]{1,0:T(8,128)(2,1)} %add_convert_fusion.refs_10_.refs_1_), channel_id=1, source_target_pairs={{0,2},{1,3},{2,0},{3,1},{4,6},{5,7},{6,4},{7,5},{8,10},{9,11},{10,... | collective-permute-start | bytes 7864328 | tf_op jit(solution)/shard_map/ppermute | solution.py:244
  139.6 59.8 %collective-permute-start.10 = (bf16[1024,1280]{1,0:T(8,128)(2,1)}, bf16[1024,1280]{1,0:T(8,128)(2,1)}, u32[]{:S(2)}, u32[]{:S(2)}) collective-permute-start(bf16[1024,1280]{1,0:T(8,128)(2,1)} %add_convert_fusion.refs_10_.refs_1_), channel_id=1, source_target_pairs={{0,4},{1,5},{2,6},{3,7},{4,0},{5,1},{6,2},{7,3},{8,12},{9,13},{10,... | collective-permute-start | bytes 7864328 | tf_op jit(solution)/shard_map/ppermute | solution.py:244
  153.0 55.3 %collective-permute-start.29 = (bf16[1024,1280]{1,0:T(8,128)(2,1)}, bf16[1024,1280]{1,0:T(8,128)(2,1)}, u32[]{:S(2)}, u32[]{:S(2)}) collective-permute-start(bf16[1024,1280]{1,0:T(8,128)(2,1)} %collective-permute-done.27.refs_1_), channel_id=1, source_target_pairs={{0,1},{1,0},{2,3},{3,2},{4,5},{5,4},{6,7},{7,6},{8,9},{9,8},{10,11... | collective-permute-start | bytes 7864328 | tf_op jit(solution)/shard_map/ppermute | solution.py:244
  153.0 83.9 %collective-permute-start.31 = (bf16[1024,1280]{1,0:T(8,128)(2,1)}, bf16[1024,1280]{1,0:T(8,128)(2,1)}, u32[]{:S(2)}, u32[]{:S(2)}) collective-permute-start(bf16[1024,1280]{1,0:T(8,128)(2,1)} %multiply_convert_fusion.refs_4_.refs_1_), channel_id=1, source_target_pairs={{0,1},{1,0},{2,3},{3,2},{4,5},{5,4},{6,7},{7,6},{8,9},{9,8},{10,11... | collective-permute-start | bytes 7864328 | tf_op jit(solution)/shard_map/ppermute | solution.py:244
  153.5 84.0 %collective-permute-start.4 = (bf16[1024,1280]{1,0:T(8,128)(2,1)}, bf16[1024,1280]{1,0:T(8,128)(2,1)}, u32[]{:S(2)}, u32[]{:S(2)}) collective-permute-start(bf16[1024,1280]{1,0:T(8,128)(2,1)} %refs_0_.3), channel_id=1, source_target_pairs={{0,1},{1,0},{2,3},{3,2},{4,5},{5,4},{6,7},{7,6},{8,9},{9,8},{10,11... | collective-permute-start | bytes 7864328 | tf_op jit(solution)/shard_map/ppermute | solution.py:244
  196.9 41.1 %collective-permute-start.32 = (bf16[1024,1280]{1,0:T(8,128)(2,1)}, bf16[1024,1280]{1,0:T(8,128)(2,1)}, u32[]{:S(2)}, u32[]{:S(2)}) collective-permute-start(bf16[1024,1280]{1,0:T(8,128)(2,1)} %collective-permute-done.30.refs_5_.refs_2_), channel_id=1, source_target_pairs={{0,1},{1,0},{2,3},{3,2},{4,5},{5,4},{6,7},{7,6},{8,9},{9,8},{10,11... | collective-permute-start | bytes 7864328 | tf_op jit(solution)/shard_map/ppermute | solution.py:244
  199.4 38.6 %collective-permute-start.2 = (bf16[512,1280]{1,0:T(8,128)(2,1)}, bf16[512,1280]{1,0:T(8,128)(2,1)}, u32[]{:S(2)}, u32[]{:S(2)}) collective-permute-start(bf16[512,1280]{1,0:T(8,128)(2,1)} %slice.54), channel_id=1, source_target_pairs={{0,4},{1,5},{2,6},{3,7},{4,0},{5,1},{6,2},{7,3},{8,12},{9,13},{10,... | collective-permute-start | bytes 3932168 | tf_op jit(solution)/shard_map/ppermute | solution.py:244
  208.3 85.5 %collective-permute-start.3 = (bf16[512,1280]{1,0:T(8,128)(2,1)}, bf16[512,1280]{1,0:T(8,128)(2,1)}, u32[]{:S(2)}, u32[]{:S(2)}) collective-permute-start(bf16[512,1280]{1,0:T(8,128)(2,1)} %slice.55), channel_id=1, source_target_pairs={{0,2},{1,3},{2,0},{3,1},{4,6},{5,7},{6,4},{7,5},{8,10},{9,11},{10,... | collective-permute-start | bytes 3932168 | tf_op jit(solution)/shard_map/ppermute | solution.py:244
  236.9 57.0 %collective-permute-start.11 = (bf16[512,1280]{1,0:T(8,128)(2,1)}, bf16[512,1280]{1,0:T(8,128)(2,1)}, u32[]{:S(2)}, u32[]{:S(2)}) collective-permute-start(bf16[512,1280]{1,0:T(8,128)(2,1)} %slice.56), channel_id=1, source_target_pairs={{0,4},{1,5},{2,6},{3,7},{4,0},{5,1},{6,2},{7,3},{8,12},{9,13},{10,... | collective-permute-start | bytes 3932168 | tf_op jit(solution)/shard_map/ppermute | solution.py:244
  237.5 63.0 %collective-permute-start.12 = (bf16[512,1280]{1,0:T(8,128)(2,1)}, bf16[512,1280]{1,0:T(8,128)(2,1)}, u32[]{:S(2)}, u32[]{:S(2)}) collective-permute-start(bf16[512,1280]{1,0:T(8,128)(2,1)} %slice.57), channel_id=1, source_target_pairs={{0,2},{1,3},{2,0},{3,1},{4,6},{5,7},{6,4},{7,5},{8,10},{9,11},{10,... | collective-permute-start | bytes 3932168 | tf_op jit(solution)/shard_map/ppermute | solution.py:244
  238.0 62.5 %collective-permute-start.5 = (bf16[1024,1280]{1,0:T(8,128)(2,1)}, bf16[1024,1280]{1,0:T(8,128)(2,1)}, u32[]{:S(2)}, u32[]{:S(2)}) collective-permute-start(bf16[1024,1280]{1,0:T(8,128)(2,1)} %collective-permute-done.refs_1_), channel_id=1, source_target_pairs={{0,1},{1,0},{2,3},{3,2},{4,5},{5,4},{6,7},{7,6},{8,9},{9,8},{10,11... | collective-permute-start | bytes 7864328 | tf_op jit(solution)/shard_map/ppermute | solution.py:244
  238.0 62.9 %collective-permute-start.6 = (bf16[1024,1280]{1,0:T(8,128)(2,1)}, bf16[1024,1280]{1,0:T(8,128)(2,1)}, u32[]{:S(2)}, u32[]{:S(2)}) collective-permute-start(bf16[1024,1280]{1,0:T(8,128)(2,1)} %collective-permute-done.1.refs_2_), channel_id=1, source_target_pairs={{0,1},{1,0},{2,3},{3,2},{4,5},{5,4},{6,7},{7,6},{8,9},{9,8},{10,11... | collective-permute-start | bytes 7864328 | tf_op jit(solution)/shard_map/ppermute | solution.py:244
  293.8 31.1 %collective-permute-start.7 = (bf16[512,1280]{1,0:T(8,128)(2,1)}, bf16[512,1280]{1,0:T(8,128)(2,1)}, u32[]{:S(2)}, u32[]{:S(2)}) collective-permute-start(bf16[512,1280]{1,0:T(8,128)(2,1)} %collective-permute-done.2.refs_3_), channel_id=1, source_target_pairs={{0,1},{1,0},{2,3},{3,2},{4,5},{5,4},{6,7},{7,6},{8,9},{9,8},{10,11... | collective-permute-start | bytes 3932168 | tf_op jit(solution)/shard_map/ppermute | solution.py:244
  293.9 31.5 %collective-permute-start.8 = (bf16[512,1280]{1,0:T(8,128)(2,1)}, bf16[512,1280]{1,0:T(8,128)(2,1)}, u32[]{:S(2)}, u32[]{:S(2)}) collective-permute-start(bf16[512,1280]{1,0:T(8,128)(2,1)} %collective-permute-done.3.refs_4_), channel_id=1, source_target_pairs={{0,1},{1,0},{2,3},{3,2},{4,5},{5,4},{6,7},{7,6},{8,9},{9,8},{10,11... | collective-permute-start | bytes 3932168 | tf_op jit(solution)/shard_map/ppermute | solution.py:244
  300.4 64.7 %collective-permute-start.13 = (bf16[1024,1280]{1,0:T(8,128)(2,1)}, bf16[1024,1280]{1,0:T(8,128)(2,1)}, u32[]{:S(2)}, u32[]{:S(2)}) collective-permute-start(bf16[1024,1280]{1,0:T(8,128)(2,1)} %add_convert_fusion.refs_10_.refs_1_), channel_id=1, source_target_pairs={{0,1},{1,0},{2,3},{3,2},{4,5},{5,4},{6,7},{7,6},{8,9},{9,8},{10,11... | collective-permute-start | bytes 7864328 | tf_op jit(solution)/shard_map/ppermute | solution.py:244
  300.5 64.6 %collective-permute-start.14 = (bf16[1024,1280]{1,0:T(8,128)(2,1)}, bf16[1024,1280]{1,0:T(8,128)(2,1)}, u32[]{:S(2)}, u32[]{:S(2)}) collective-permute-start(bf16[1024,1280]{1,0:T(8,128)(2,1)} %collective-permute-done.9.refs_11_.refs_2_), channel_id=1, source_target_pairs={{0,1},{1,0},{2,3},{3,2},{4,5},{5,4},{6,7},{7,6},{8,9},{9,8},{10,11... | collective-permute-start | bytes 7864328 | tf_op jit(solution)/shard_map/ppermute | solution.py:244
  301.0 64.2 %collective-permute-start.15 = (bf16[1024,1280]{1,0:T(8,128)(2,1)}, bf16[1024,1280]{1,0:T(8,128)(2,1)}, u32[]{:S(2)}, u32[]{:S(2)}) collective-permute-start(bf16[1024,1280]{1,0:T(8,128)(2,1)} %collective-permute-done.10.refs_12_.refs_3_), channel_id=1, source_target_pairs={{0,1},{1,0},{2,3},{3,2},{4,5},{5,4},{6,7},{7,6},{8,9},{9,8},{10,11... | collective-permute-start | bytes 7864328 | tf_op jit(solution)/shard_map/ppermute | solution.py:244
  324.9 40.2 %collective-permute-start.16 = (bf16[512,1280]{1,0:T(8,128)(2,1)}, bf16[512,1280]{1,0:T(8,128)(2,1)}, u32[]{:S(2)}, u32[]{:S(2)}) collective-permute-start(bf16[512,1280]{1,0:T(8,128)(2,1)} %collective-permute-done.11.refs_13_.refs_4_), channel_id=1, source_target_pairs={{0,1},{1,0},{2,3},{3,2},{4,5},{5,4},{6,7},{7,6},{8,9},{9,8},{10,11... | collective-permute-start | bytes 3932168 | tf_op jit(solution)/shard_map/ppermute | solution.py:244
  325.4 39.7 %collective-permute-start.17 = (bf16[512,1280]{1,0:T(8,128)(2,1)}, bf16[512,1280]{1,0:T(8,128)(2,1)}, u32[]{:S(2)}, u32[]{:S(2)}) collective-permute-start(bf16[512,1280]{1,0:T(8,128)(2,1)} %collective-permute-done.12.refs_14_.refs_5_), channel_id=1, source_target_pairs={{0,1},{1,0},{2,3},{3,2},{4,5},{5,4},{6,7},{7,6},{8,9},{9,8},{10,11... | collective-permute-start | bytes 3932168 | tf_op jit(solution)/shard_map/ppermute | solution.py:244
  440.9 46.7 %collective-permute-start.21 = (f32[320,640]{1,0:T(8,128)S(1)}, f32[320,640]{1,0:T(8,128)}, u32[]{:S(2)}, u32[]{:S(2)}) collective-permute-start(f32[320,640]{1,0:T(8,128)S(1)} %get-tuple-element.27), channel_id=1, source_target_pairs={{24,16},{25,17},{26,18},{27,19},{28,20},{29,21},{30,22},{31,23}} | collective-permute-start | bytes 2457608 | tf_op jit(solution)/shard_map/ppermute | solution.py:244
  442.5 57.2 %collective-permute-start.18 = (f32[320,640]{1,0:T(8,128)}, f32[320,640]{1,0:T(8,128)}, u32[]{:S(2)}, u32[]{:S(2)}) collective-permute-start(f32[320,640]{1,0:T(8,128)} %get-tuple-element.24), channel_id=1, source_target_pairs={{0,8},{1,9},{2,10},{3,11},{4,12},{5,13},{6,14},{7,15}} | collective-permute-start | bytes 2457608 | tf_op jit(solution)/shard_map/ppermute | solution.py:244
  444.8 47.3 %collective-permute-start.53 = (f32[2,2,160,384]{3,2,1,0:T(8,128)}, f32[2,2,160,384]{3,2,1,0:T(8,128)}, u32[]{:S(2)}, u32[]{:S(2)}) collective-permute-start(f32[2,2,160,384]{3,2,1,0:T(8,128)} %dynamic-slice_bitcast_fusion.3), channel_id=1, source_target_pairs={{0,16},{1,17},{2,18},{3,19},{4,20},{5,21},{6,22},{7,23},{8,24},{9,... | collective-permute-start | bytes 2949128 | tf_op jit(solution)/shard_map/ppermute | solution.py:244
  450.5 44.3 %collective-permute-start.50 = (f32[2,2,160,384]{3,2,1,0:T(8,128)}, f32[2,2,160,384]{3,2,1,0:T(8,128)}, u32[]{:S(2)}, u32[]{:S(2)}) collective-permute-start(f32[2,2,160,384]{3,2,1,0:T(8,128)} %dynamic-slice_bitcast_fusion.4), channel_id=1, source_target_pairs={{0,4},{1,5},{2,6},{3,7},{4,0},{5,1},{6,2},{7,3},{8,12},{9,13},{10,... | collective-permute-start | bytes 2949128 | tf_op jit(solution)/shard_map/ppermute | solution.py:244
  453.2 67.7 %collective-permute-start.47 = (f32[2,2,160,512]{3,2,1,0:T(8,128)}, f32[2,2,160,512]{3,2,1,0:T(8,128)}, u32[]{:S(2)}, u32[]{:S(2)}) collective-permute-start(f32[2,2,160,512]{3,2,1,0:T(8,128)} %dynamic-slice_bitcast_fusion.2), channel_id=1, source_target_pairs={{0,2},{1,3},{2,0},{3,1},{4,6},{5,7},{6,4},{7,5},{8,10},{9,11},{10,... | collective-permute-start | bytes 3932168 | tf_op jit(solution)/shard_map/ppermute | solution.py:244
  487.6 13.6 %collective-permute-start.44 = (f32[160,1280]{1,0:T(8,128)S(1)}, f32[160,1280]{1,0:T(8,128)S(1)}, u32[]{:S(2)}, u32[]{:S(2)}) collective-permute-start(f32[160,1280]{1,0:T(8,128)S(1)} %get-tuple-element.36), channel_id=1, source_target_pairs={{24,16},{25,17},{26,18},{27,19},{28,20},{29,21},{30,22},{31,23}} | collective-permute-start | bytes 2457608 | tf_op jit(solution)/shard_map/ppermute | solution.py:244
  492.1 21.3 %collective-permute-start.41 = (f32[160,1280]{1,0:T(8,128)S(1)}, f32[160,1280]{1,0:T(8,128)S(1)}, u32[]{:S(2)}, u32[]{:S(2)}) collective-permute-start(f32[160,1280]{1,0:T(8,128)S(1)} %get-tuple-element.33), channel_id=1, source_target_pairs={{0,8},{1,9},{2,10},{3,11},{4,12},{5,13},{6,14},{7,15}} | collective-permute-start | bytes 2457608 | tf_op jit(solution)/shard_map/ppermute | solution.py:244
  494.8 37.7 %collective-permute-start.33 = (f32[2,2,2,2,40,640]{5,4,3,2,1,0:T(8,128)}, f32[2,2,2,2,40,640]{5,4,3,2,1,0:T(8,128)}, u32[]{:S(2)}, u32[]{:S(2)}) collective-permute-start(f32[2,2,2,2,40,640]{5,4,3,2,1,0:T(8,128)} %dynamic-slice_bitcast_fusion.1), channel_id=1, source_target_pairs={{0,4},{1,5},{2,6},{3,7},{4,0},{5,1},{6,2},{7,3},{8,12},{9,13},{10,... | collective-permute-start | bytes 4915208 | tf_op jit(solution)/shard_map/ppermute | solution.py:244
  499.7 24.5 %collective-permute-start.54 = (f32[2,160,384]{2,1,0:T(8,128)}, f32[2,160,384]{2,1,0:T(8,128)}, u32[]{:S(2)}, u32[]{:S(2)}) collective-permute-start(f32[2,160,384]{2,1,0:T(8,128)} %dynamic-slice_bitcast_fusion.22), channel_id=1, source_target_pairs={{0,2},{1,3},{2,0},{3,1},{4,6},{5,7},{6,4},{7,5},{8,10},{9,11},{10,... | collective-permute-start | bytes 1474568 | tf_op jit(solution)/shard_map/ppermute | solution.py:244
  501.2 27.6 %collective-permute-start.51 = (f32[2,160,384]{2,1,0:T(8,128)}, f32[2,160,384]{2,1,0:T(8,128)}, u32[]{:S(2)}, u32[]{:S(2)}) collective-permute-start(f32[2,160,384]{2,1,0:T(8,128)} %dynamic-slice_bitcast_fusion.23), channel_id=1, source_target_pairs={{0,2},{1,3},{2,0},{3,1},{4,6},{5,7},{6,4},{7,5},{8,10},{9,11},{10,... | collective-permute-start | bytes 1474568 | tf_op jit(solution)/shard_map/ppermute | solution.py:244
  514.3 49.7 %collective-permute-start.36 = (f32[2,2,2,2,40,640]{5,4,3,2,1,0:T(8,128)}, f32[2,2,2,2,40,640]{5,4,3,2,1,0:T(8,128)}, u32[]{:S(2)}, u32[]{:S(2)}) collective-permute-start(f32[2,2,2,2,40,640]{5,4,3,2,1,0:T(8,128)} %dynamic-slice_bitcast_fusion), channel_id=1, source_target_pairs={{0,2},{1,3},{2,0},{3,1},{4,6},{5,7},{6,4},{7,5},{8,10},{9,11},{10,... | collective-permute-start | bytes 4915208 | tf_op jit(solution)/shard_map/ppermute | solution.py:244
  520.7 25.0 %copy-start.2 = (f32[2,2,2,2,2,40,640]{6,5,4,3,2,1,0:T(8,128)S(1)}, f32[2,2,2,2,2,40,640]{6,5,4,3,2,1,0:T(8,128)}, u32[]{:S(2)}) copy-start(f32[2,2,2,2,2,40,640]{6,5,4,3,2,1,0:T(8,128)} %get-tuple-element.41) | copy-start | bytes 9830404
  520.9 23.3 %collective-permute-start.22 = (f32[320,640]{1,0:T(8,128)S(1)}, f32[320,640]{1,0:T(8,128)S(1)}, u32[]{:S(2)}, u32[]{:S(2)}) collective-permute-start(f32[320,640]{1,0:T(8,128)S(1)} %add.306), channel_id=1, source_target_pairs={{16,8},{17,9},{18,10},{19,11},{20,12},{21,13},{22,14},{23,15},{24,... | collective-permute-start | bytes 2457608 | tf_op jit(solution)/shard_map/ppermute | solution.py:244
  524.1 23.3 %copy-start.16 = (f32[320,640]{1,0:T(8,128)S(1)}, f32[320,640]{1,0:T(8,128)}, u32[]{:S(2)}) copy-start(f32[320,640]{1,0:T(8,128)} %get-tuple-element.25) | copy-start | bytes 2457604
  524.2 23.3 %collective-permute-start.19 = (f32[320,640]{1,0:T(8,128)S(1)}, f32[320,640]{1,0:T(8,128)S(1)}, u32[]{:S(2)}, u32[]{:S(2)}) collective-permute-start(f32[320,640]{1,0:T(8,128)S(1)} %add.303), channel_id=1, source_target_pairs={{0,8},{1,9},{2,10},{3,11},{4,12},{5,13},{6,14},{7,15},{8,16},{9,17... | collective-permute-start | bytes 2457608 | tf_op jit(solution)/shard_map/ppermute | solution.py:244
  528.9 35.0 %collective-permute-start.45 = (f32[160,1280]{1,0:T(8,128)S(1)}, f32[160,1280]{1,0:T(8,128)S(1)}, u32[]{:S(2)}, u32[]{:S(2)}) collective-permute-start(f32[160,1280]{1,0:T(8,128)S(1)} %add.330), channel_id=1, source_target_pairs={{16,8},{17,9},{18,10},{19,11},{20,12},{21,13},{22,14},{23,15},{24,... | collective-permute-start | bytes 2457608 | tf_op jit(solution)/shard_map/ppermute | solution.py:244
  531.3 17.7 %copy-start.15 = (f32[320,640]{1,0:T(8,128)S(1)}, f32[320,640]{1,0:T(8,128)}, u32[]{:S(2)}) copy-start(f32[320,640]{1,0:T(8,128)} %get-tuple-element.22) | copy-start | bytes 2457604
  532.5 31.4 %copy-start.18 = (f32[160,1280]{1,0:T(8,128)S(1)}, f32[160,1280]{1,0:T(8,128)}, u32[]{:S(2)}) copy-start(f32[160,1280]{1,0:T(8,128)} %get-tuple-element.34) | copy-start | bytes 2457604
  532.5 41.3 %collective-permute-start.42 = (f32[160,1280]{1,0:T(8,128)S(1)}, f32[160,1280]{1,0:T(8,128)S(1)}, u32[]{:S(2)}, u32[]{:S(2)}) collective-permute-start(f32[160,1280]{1,0:T(8,128)S(1)} %add.327), channel_id=1, source_target_pairs={{0,8},{1,9},{2,10},{3,11},{4,12},{5,13},{6,14},{7,15},{8,16},{9,17... | collective-permute-start | bytes 2457608 | tf_op jit(solution)/shard_map/ppermute | solution.py:244
  544.2 31.2 %collective-permute-start.48 = (f32[2,160,512]{2,1,0:T(8,128)S(1)}, f32[2,160,512]{2,1,0:T(8,128)S(1)}, u32[]{:S(2)}, u32[]{:S(2)}) collective-permute-start(f32[2,160,512]{2,1,0:T(8,128)S(1)} %dynamic-slice_bitcast_fusion.21), channel_id=1, source_target_pairs={{0,4},{1,5},{2,6},{3,7},{4,0},{5,1},{6,2},{7,3},{8,12},{9,13},{10,... | collective-permute-start | bytes 1966088 | tf_op jit(solution)/shard_map/ppermute | solution.py:244
  547.5 30.0 %collective-permute-start.55 = (f32[160,384]{1,0:T(8,128)S(1)}, f32[160,384]{1,0:T(8,128)S(1)}, u32[]{:S(2)}, u32[]{:S(2)}) collective-permute-start(f32[160,384]{1,0:T(8,128)S(1)} %dynamic-slice_bitcast_fusion.28), channel_id=1, source_target_pairs={{0,4},{1,5},{2,6},{3,7},{4,0},{5,1},{6,2},{7,3},{8,12},{9,13},{10,... | collective-permute-start | bytes 737288 | tf_op jit(solution)/shard_map/ppermute | solution.py:244
  549.1 26.2 %copy-start.17 = (f32[160,1280]{1,0:T(8,128)S(1)}, f32[160,1280]{1,0:T(8,128)}, u32[]{:S(2)}) copy-start(f32[160,1280]{1,0:T(8,128)} %get-tuple-element.31) | copy-start | bytes 2457604
  563.9 17.7 %collective-permute-start.52 = (f32[160,384]{1,0:T(8,128)S(1)}, f32[160,384]{1,0:T(8,128)S(1)}, u32[]{:S(2)}, u32[]{:S(2)}) collective-permute-start(f32[160,384]{1,0:T(8,128)S(1)} %dynamic-slice_bitcast_fusion.29), channel_id=1, source_target_pairs={{0,16},{1,17},{2,18},{3,19},{4,20},{5,21},{6,22},{7,23},{8,24},{9,... | collective-permute-start | bytes 737288 | tf_op jit(solution)/shard_map/ppermute | solution.py:244
  564.0 56.8 %collective-permute-start.34 = (f32[2,2,2,40,640]{4,3,2,1,0:T(8,128)S(1)}, f32[2,2,2,40,640]{4,3,2,1,0:T(8,128)S(1)}, u32[]{:S(2)}, u32[]{:S(2)}) collective-permute-start(f32[2,2,2,40,640]{4,3,2,1,0:T(8,128)S(1)} %dynamic-slice_bitcast_fusion.13), channel_id=1, source_target_pairs={{0,2},{1,3},{2,0},{3,1},{4,6},{5,7},{6,4},{7,5},{8,10},{9,11},{10,... | collective-permute-start | bytes 2457608 | tf_op jit(solution)/shard_map/ppermute | solution.py:244
  573.8 49.1 %collective-permute-start.37 = (f32[2,2,2,40,640]{4,3,2,1,0:T(8,128)S(1)}, f32[2,2,2,40,640]{4,3,2,1,0:T(8,128)S(1)}, u32[]{:S(2)}, u32[]{:S(2)}) collective-permute-start(f32[2,2,2,40,640]{4,3,2,1,0:T(8,128)S(1)} %dynamic-slice_bitcast_fusion.12), channel_id=1, source_target_pairs={{0,4},{1,5},{2,6},{3,7},{4,0},{5,1},{6,2},{7,3},{8,12},{9,13},{10,... | collective-permute-start | bytes 2457608 | tf_op jit(solution)/shard_map/ppermute | solution.py:244
  575.4 47.7 %collective-permute-start.23 = (f32[320,640]{1,0:T(8,128)S(1)}, f32[320,640]{1,0:T(8,128)S(1)}, u32[]{:S(2)}, u32[]{:S(2)}) collective-permute-start(f32[320,640]{1,0:T(8,128)S(1)} %add.307), channel_id=1, source_target_pairs={{8,0},{9,1},{10,2},{11,3},{12,4},{13,5},{14,6},{15,7},{16,8},{17,9... | collective-permute-start | bytes 2457608 | tf_op jit(solution)/shard_map/ppermute | solution.py:244
  577.5 48.6 %copy-start.13 = (f32[320,640]{1,0:T(8,128)S(1)}, f32[320,640]{1,0:T(8,128)}, u32[]{:S(2)}) copy-start(f32[320,640]{1,0:T(8,128)} %get-tuple-element.21) | copy-start | bytes 2457604
  577.5 19.5 %collective-permute-start.49 = (f32[160,512]{1,0:T(8,128)S(1)}, f32[160,512]{1,0:T(8,128)S(1)}, u32[]{:S(2)}, u32[]{:S(2)}) collective-permute-start(f32[160,512]{1,0:T(8,128)S(1)} %dynamic-slice_bitcast_fusion.27), channel_id=1, source_target_pairs={{0,16},{1,17},{2,18},{3,19},{4,20},{5,21},{6,22},{7,23},{8,24},{9,... | collective-permute-start | bytes 983048 | tf_op jit(solution)/shard_map/ppermute | solution.py:244
  581.6 44.5 %collective-permute-start.20 = (f32[320,640]{1,0:T(8,128)S(1)}, f32[320,640]{1,0:T(8,128)S(1)}, u32[]{:S(2)}, u32[]{:S(2)}) collective-permute-start(f32[320,640]{1,0:T(8,128)S(1)} %add.304), channel_id=1, source_target_pairs={{0,8},{1,9},{2,10},{3,11},{4,12},{5,13},{6,14},{7,15},{8,16},{9,17... | collective-permute-start | bytes 2457608 | tf_op jit(solution)/shard_map/ppermute | solution.py:244
  597.0 60.0 %collective-permute-start.46 = (f32[160,1280]{1,0:T(8,128)S(1)}, f32[160,1280]{1,0:T(8,128)S(1)}, u32[]{:S(2)}, u32[]{:S(2)}) collective-permute-start(f32[160,1280]{1,0:T(8,128)S(1)} %add.331), channel_id=1, source_target_pairs={{8,0},{9,1},{10,2},{11,3},{12,4},{13,5},{14,6},{15,7},{16,8},{17,9... | collective-permute-start | bytes 2457608 | tf_op jit(solution)/shard_map/ppermute | solution.py:244
  620.8 36.3 %collective-permute-start.43 = (f32[160,1280]{1,0:T(8,128)S(1)}, f32[160,1280]{1,0:T(8,128)S(1)}, u32[]{:S(2)}, u32[]{:S(2)}) collective-permute-start(f32[160,1280]{1,0:T(8,128)S(1)} %add.328), channel_id=1, source_target_pairs={{0,8},{1,9},{2,10},{3,11},{4,12},{5,13},{6,14},{7,15},{8,16},{9,17... | collective-permute-start | bytes 2457608 | tf_op jit(solution)/shard_map/ppermute | solution.py:244
  622.9 34.2 %copy-start.14 = (f32[160,1280]{1,0:T(8,128)S(1)}, f32[160,1280]{1,0:T(8,128)}, u32[]{:S(2)}) copy-start(f32[160,1280]{1,0:T(8,128)} %get-tuple-element.30) | copy-start | bytes 2457604
  622.9 29.6 %collective-permute-start.35 = (f32[2,2,40,640]{3,2,1,0:T(8,128)S(1)}, f32[2,2,40,640]{3,2,1,0:T(8,128)S(1)}, u32[]{:S(2)}, u32[]{:S(2)}) collective-permute-start(f32[2,2,40,640]{3,2,1,0:T(8,128)S(1)} %dynamic-slice_bitcast_fusion.25), channel_id=1, source_target_pairs={{0,16},{1,17},{2,18},{3,19},{4,20},{5,21},{6,22},{7,23},{8,24},{9,... | collective-permute-start | bytes 1228808 | tf_op jit(solution)/shard_map/ppermute | solution.py:244
  623.1 33.7 %collective-permute-start.38 = (f32[2,2,40,640]{3,2,1,0:T(8,128)S(1)}, f32[2,2,40,640]{3,2,1,0:T(8,128)S(1)}, u32[]{:S(2)}, u32[]{:S(2)}) collective-permute-start(f32[2,2,40,640]{3,2,1,0:T(8,128)S(1)} %dynamic-slice_bitcast_fusion.24), channel_id=1, source_target_pairs={{0,16},{1,17},{2,18},{3,19},{4,20},{5,21},{6,22},{7,23},{8,24},{9,... | collective-permute-start | bytes 1228808 | tf_op jit(solution)/shard_map/ppermute | solution.py:244
  626.3 31.0 %collective-permute-start.24 = (f32[2,2,40,640]{3,2,1,0:T(8,128)S(1)}, f32[2,2,40,640]{3,2,1,0:T(8,128)S(1)}, u32[]{:S(2)}, u32[]{:S(2)}) collective-permute-start(f32[2,2,40,640]{3,2,1,0:T(8,128)S(1)} %dynamic-slice_bitcast_fusion.26), channel_id=1, source_target_pairs={{0,4},{1,5},{2,6},{3,7},{4,0},{5,1},{6,2},{7,3},{8,12},{9,13},{10,... | collective-permute-start | bytes 1228808 | tf_op jit(solution)/shard_map/ppermute | solution.py:244
  657.0 8.0 %collective-permute-start.39 = (f32[2,40,1280]{2,1,0:T(8,128)S(1)}, f32[2,40,1280]{2,1,0:T(8,128)S(1)}, u32[]{:S(2)}, u32[]{:S(2)}) collective-permute-start(f32[2,40,1280]{2,1,0:T(8,128)S(1)} %fusion.79), channel_id=1, source_target_pairs={{0,8},{1,9},{2,10},{3,11},{4,12},{5,13},{6,14},{7,15},{8,0},{9,1},... | collective-permute-start | bytes 1228808 | tf_op jit(solution)/shard_map/ppermute | solution.py:244
  657.4 9.1 %collective-permute-start.25 = (f32[2,2,40,640]{3,2,0,1:T(8,128)S(1)}, f32[2,2,40,640]{3,2,0,1:T(8,128)S(1)}, u32[]{:S(2)}, u32[]{:S(2)}) collective-permute-start(f32[2,2,40,640]{3,2,0,1:T(8,128)S(1)} %fusion.87), channel_id=1, source_target_pairs={{0,2},{1,3},{2,0},{3,1},{4,6},{5,7},{6,4},{7,5},{8,10},{9,11},{10,... | collective-permute-start | bytes 1228808 | tf_op jit(solution)/shard_map/ppermute | solution.py:244
  665.1 2.7 collective-permute-start.40
  667.3 6.0 collective-permute-start.26
  (17 other events, 135.6 us)
